TPU v7x, 32 devices: a whole 2x2x4 slice. The times are simulated.
32 devices in a mesh: groups: 2 (over y), seq: 4 (over x, core), qset: 4 (over z).
Axes of the slice: x: 2, y: 2, z: 4, core: 2. Of those that a mesh axis runs over, the one named last changes fastest.
Arguments:
- states: bfloat16 [8, 4, 128, 4096], P(('groups', 'qset'), 'seq'), parts along dimension 0, may hold values from -7 to 7
- enc_gain: bfloat16 [4096], replicated, may hold values from 0.25 to 1.75
- dec_states: bfloat16 [16, 64, 4096], P(('groups', 'qset')), parts along dimension 0, may hold values from -7 to 7
- dec_gain: bfloat16 [4096], replicated, may hold values from 0.25 to 1.75
- query_weight: bfloat16 [4096, 4096], P(None, 'seq'), may hold values from -0.375 to 0.375
- key_value_weight: bfloat16 [4096, 2, 4096], P(None, None, 'seq'), may hold values from -0.0625 to 0.0625
- out_weight: bfloat16 [4096, 4096], P('seq'), may hold values from -0.75 to 0.75
- question_of: int32 [8, 4, 1], P('groups'), parts along dimension 0, may hold values from 0 to 7; in each aligned block of 4 rows (0 to 3, 4 to 7, ..., all dimensions but the last counted through in order) at most 2 rows name the same one
Outputs:
- mixed: bfloat16 [16, 64, 4096], P(('groups', 'qset'), None, 'seq'), parts along dimension 0
There are 2 independent parts, one for each index of `groups`. A program takes and returns all parts, laid end to end along the dimension named above; an argument that names none is the same for every part. Nothing has to cross between parts.
Inputs may be any that keep to these rules, and one draw needn't show every extreme that they name: `question_of`: within each index of the first dimension (one source group of 4 passages) at most 2 passages name the same question, and exactly 2 do for some question in some groups; every question is named by at least one passage.
All inputs are finite; a program needn't handle non-finite values.
Results may differ from a plain program's by a relative error of at most 0.014.
The roundings to bfloat16 on the way count: a program that leaves them out, or rounds other values in their place, can miss the bound.
Values may be sent and summed in bfloat16 or wider, within the bound.
A program may use at most 128 MiB of HBM per device.

v0:
```python
import functools
import jax
import jax.numpy as jnp
from jax import lax
from jax.experimental import pallas as pl
from jax.experimental.pallas import tpu as pltpu
from jax.sharding import PartitionSpec as P

HD = 64
EPSILON = 1e-06
DEAD = -1e30
CHUNKS = 4
F32 = jnp.float32
BF16 = jnp.bfloat16


def norm_rows(load, store, gain, rows):
    step = 16

    def one(i, carry):
        at = pl.ds(pl.multiple_of(i * step, step), step)
        x = load(at).astype(F32)
        ms = jnp.mean(x * x, axis=-1, keepdims=True)
        store(at, (x * lax.rsqrt(ms + EPSILON) * gain).astype(BF16))
        return carry

    lax.fori_loop(0, rows // step, one, 0)


def kernel(
    cfg, qo, states, enc_gain, dec_states, dec_gain, qw, kvw, ow, out,
    gat, qw_v, raw, pulled, kv_v, ow_v, xn, kvs, qall, a_s, e_s, psend, ssend, precv, srecv,
    att, oacc, rsend, rpart, rx, rown,
    local_sem, raw_sem, xs_send, xs_recv, q_send, q_recv, p_send, p_recv, s_send, s_recv,
    d_send, d_recv, r_send, r_recv,
):
    n_seq, nz, nlq, plen, dlen, width, cols = cfg
    nx = n_seq // 2
    npairs = cols // 128
    rows = nlq * dlen
    nch = 4 if npairs % 4 == 0 else npairs
    pc = npairs // nch
    cw = pc * 128
    me = lax.axis_index("seq")
    z = lax.axis_index("qset")
    x = me // 2
    c = lax.rem(me, 2)
    partner = x * 2 + (1 - c)

    def seq_of(dx, core):
        return lax.rem(x + dx, nx) * 2 + core

    own_copy = pltpu.make_async_copy(states, gat.at[me], local_sem.at[0])
    own_copy.start()
    qw_copy = pltpu.make_async_copy(qw, qw_v, local_sem.at[1])
    qw_copy.start()
    nblocks = cols // 128
    slots = raw.shape[0]

    def raw_copy(b):
        return pltpu.make_async_copy(
            kvw.at[:, :, pl.ds(b * 128, 128)], raw.at[b % slots], raw_sem.at[b % slots]
        )

    for b in range(min(slots, nblocks)):
        raw_copy(b).start()
    ow_copy = pltpu.make_async_copy(ow, ow_v, local_sem.at[3])

    barrier = pltpu.get_barrier_semaphore()
    for dx in range(1, nx):
        pl.semaphore_signal(barrier, 1, device_id={"seq": seq_of(dx, c)})
    pl.semaphore_signal(barrier, 1, device_id={"seq": partner})
    for dz in range(1, nz):
        pl.semaphore_signal(barrier, 1, device_id={"qset": lax.rem(z + dz, nz)})
    pl.semaphore_wait(barrier, nx - 1 + 1 + nz - 1)

    own_copy.wait()
    crows = plen // CHUNKS

    def state_copy(slot, ch, to, send_sem):
        part = gat.at[slot, pl.ds(ch * crows, crows)]
        return pltpu.make_async_remote_copy(
            src_ref=part, dst_ref=part, send_sem=send_sem,
            recv_sem=xs_recv.at[slot, ch], device_id={"seq": to},
        )

    pending = []
    for ch in range(CHUNKS):
        for dx in range(1, nx):
            cp = state_copy(me, ch, seq_of(dx, c), xs_send.at[0, dx, ch])
            cp.start()
            pending.append(cp)
        cp = state_copy(me, ch, partner, xs_send.at[0, 0, ch])
        cp.start()
        pending.append(cp)

    dg = dec_gain[...].astype(F32).reshape(1, width)
    eg = enc_gain[...].astype(F32).reshape(1, width)

    def put_xn(base):
        def put(at, v):
            xn[pl.ds(pl.multiple_of(base + at.start, 16), at.size), :] = v
        return put

    norm_rows(lambda at: dec_states[at, :], put_xn(0), dg, rows)
    qw_copy.wait()
    ow_copy.start()
    tile = min(256, cols)

    def q_tile(i, carry):
        at = pl.ds(pl.multiple_of(i * tile, tile), tile)
        r = jnp.dot(xn[:rows, :], qw_v[:, at], preferred_element_type=F32).astype(BF16)
        for lq in range(nlq):
            qall[z * nlq + lq, :, at] = r[lq * dlen:(lq + 1) * dlen]
        return carry

    lax.fori_loop(0, cols // tile, q_tile, 0)
    own_q = qall.at[pl.ds(z * nlq, nlq)]
    for dz in range(1, nz):
        cp = pltpu.make_async_remote_copy(
            src_ref=own_q, dst_ref=own_q, send_sem=q_send.at[dz],
            recv_sem=q_recv.at[z], device_id={"qset": lax.rem(z + dz, nz)},
        )
        cp.start()
        pending.append(cp)

    def wait_slot(slot, ch):
        state_copy(slot, ch, partner, xs_send.at[0, 0, 0]).wait_recv()

    def project(xi, start, count):
        for k in range(2):
            norm_rows(
                lambda at: gat[xi * 2 + k, pl.ds(pl.multiple_of(start + at.start, 16), at.size), :],
                put_xn(k * count), eg, count,
            )

        def kv_tile(i, carry):
            at = pl.ds(pl.multiple_of(i * tile, tile), tile)
            r = jnp.dot(
                xn[:2 * count, :], kv_v[:, at], preferred_element_type=F32
            ).astype(BF16)
            for k in range(2):
                kvs[xi, pl.ds(k * plen + start, count), at] = r[k * count:(k + 1) * count]
            return carry

        lax.fori_loop(0, 2 * cols // tile, kv_tile, 0)

    def forward(ch):
        for dx in range(1, nx):
            slot = seq_of(dx, c)
            wait_slot(slot, ch)
            cp = state_copy(slot, ch, partner, xs_send.at[1, dx, ch])
            cp.start()
            pending.append(cp)

    half = pulled.shape[0] // 2
    for b in range(nblocks):
        raw_copy(b).wait()
        flat = raw.at[b % slots].reshape(2 * width, 128)

        def pull(i, carry):
            pulled[...] = flat[pl.ds(pl.multiple_of(i * 2 * half, 2 * half), 2 * half), :].astype(F32)
            at = pl.ds(pl.multiple_of(i * half, half), half)
            kv_v[at, pl.ds(b * 128, 128)] = pulled[pl.ds(0, half, stride=2), :].astype(BF16)
            kv_v[at, pl.ds(cols + b * 128, 128)] = pulled[pl.ds(1, half, stride=2), :].astype(BF16)
            return carry

        lax.fori_loop(0, width // half, pull, 0)
        if b + slots < nblocks:
            raw_copy(b + slots).start()
        if b == nblocks // 2:
            forward(0)

    for ch in range(CHUNKS):
        wait_slot(partner, ch)
    forward(1)
    project(x, 0, plen)
    forward(2)
    part = plen // 2
    for dx in range(1, nx):
        for ch in range(CHUNKS // 2):
            wait_slot(seq_of(dx, 1 - c), ch)
        project(lax.rem(x + dx, nx), 0, part)
    forward(3)
    for dx in range(1, nx):
        for ch in range(CHUNKS // 2, CHUNKS):
            wait_slot(seq_of(dx, 1 - c), ch)
        project(lax.rem(x + dx, nx), part, part)

    for dz in range(1, nz):
        zs = lax.rem(z + dz, nz)
        src = qall.at[pl.ds(zs * nlq, nlq)]
        pltpu.make_async_remote_copy(
            src_ref=src, dst_ref=src, send_sem=q_send.at[0],
            recv_sem=q_recv.at[zs], device_id={"qset": zs},
        ).wait_recv()

    low = lax.broadcasted_iota(jnp.int32, (dlen, 128), 1) < HD
    lane = lax.broadcasted_iota(jnp.int32, (dlen, 128), 1)

    groups = dlen // 8

    def attend(g, p):
        qp = qall[qo[z, p], :, pl.ds(g * cw, cw)]
        xi = p // 2
        at = pl.ds(pl.multiple_of(lax.rem(p, 2) * plen, plen), plen)
        for i in range(pc):
            j = g * pc + i
            q = qp[:, i * 128:(i + 1) * 128]
            zero = jnp.zeros_like(q)
            q2 = jnp.concatenate([jnp.where(low, q, zero), jnp.where(low, zero, q)], axis=0)
            k = kvs[xi, at, pl.ds(j * 128, 128)]
            v = kvs[xi, at, pl.ds(cols + j * 128, 128)]
            s = lax.dot_general(q2, k, (((1,), (1,)), ((), ())), preferred_element_type=F32)
            m = jnp.max(s, axis=-1, keepdims=True)
            w = jnp.exp(s - m)
            l = jnp.sum(w, axis=-1, keepdims=True)
            o = jnp.dot(w.astype(BF16), v, preferred_element_type=F32) / l
            e = jnp.broadcast_to(m + jnp.log(l), o.shape)
            a_s[p, :, pl.ds(i * 128, 128)] = jnp.where(low, o[:dlen], o[dlen:])
            e_s[p, :, pl.ds(i * 128, 128)] = jnp.where(low, e[:dlen], e[dlen:])

    def exchange(g, dz, sender):
        zs = lax.rem(z + dz, nz)
        to = z if sender else zs
        return [
            pltpu.make_async_remote_copy(
                src_ref=src.at[g, dz], dst_ref=dst.at[g, to], send_sem=ss.at[g, dz],
                recv_sem=rs.at[g, to], device_id={"qset": zs},
            )
            for src, dst, ss, rs in (
                (ssend, srecv, s_send, s_recv), (psend, precv, p_send, p_recv),
            )
        ]

    for g in range(nch):
        lax.fori_loop(0, n_seq, lambda p, carry: (attend(g, p), carry)[1], 0, unroll=4)
        for dz in list(range(1, nz)) + [0]:
            dest = lax.rem(z + dz, nz)
            packed = jnp.zeros((dlen, 128), F32)
            for lq in range(nlq):
                question = dest * nlq + lq
                first = jnp.int32(0)
                second = jnp.int32(0)
                count = jnp.int32(0)
                for p in range(n_seq):
                    hit = qo[z, p] == question
                    first = jnp.where(hit & (count == 0), p, first)
                    second = jnp.where(hit & (count == 1), p, second)
                    count = count + hit.astype(jnp.int32)
                for i in range(pc):
                    at = pl.ds(i * 128, 128)
                    e1 = jnp.where(count >= 1, e_s[first, :, at], DEAD)
                    e2 = jnp.where(count >= 2, e_s[second, :, at], DEAD)
                    top = jnp.maximum(e1, e2)
                    w1 = jnp.exp(e1 - top)
                    w2 = jnp.exp(e2 - top)
                    tot = w1 + w2
                    a = (w1 * a_s[first, :, at] + w2 * a_s[second, :, at]) / tot
                    a = jnp.where(count >= 1, a, 0.0).astype(BF16)
                    le = jnp.where(count >= 1, top + jnp.log(tot), DEAD)
                    packed = jnp.where((lane & (HD - 1)) == lq * pc + i, le, packed)
                    if dz == 0:
                        precv[g, z, pl.ds(lq * dlen, dlen), at] = a
                    else:
                        psend[g, dz, pl.ds(lq * dlen, dlen), at] = a
            tight = jnp.zeros((8, 128), F32)
            for t in range(groups):
                piece8 = packed[t * 8:(t + 1) * 8]
                tight = tight + (pltpu.roll(piece8, t * 8, 1) if t else piece8)
            if dz == 0:
                srecv[g, z] = tight
            else:
                ssend[g, dz] = tight
                for cp in exchange(g, dz, True):
                    cp.start()
                    pending.append(cp)
    ow_copy.wait()
    otile = min(256, width // n_seq)
    for g in range(nch):
        for dz in range(1, nz):
            for cp in exchange(g, dz, False):
                cp.wait_recv()
        spread = []
        for zs in range(nz):
            t8 = srecv[g, zs]
            spread.append(jnp.concatenate(
                [pltpu.roll(t8, 128 - t * 8, 1) if t else t8 for t in range(groups)], axis=0))
        for lq in range(nlq):
            for i in range(pc):
                at = pl.ds(i * 128, 128)
                n = lq * pc + i
                es = [jnp.where(low, t[:, n:n + 1], t[:, HD + n:HD + n + 1]) for t in spread]
                top = functools.reduce(jnp.maximum, es)
                tot = jnp.zeros((dlen, 128), F32)
                acc = jnp.zeros((dlen, 128), F32)
                for zs in range(nz):
                    w = jnp.exp(es[zs] - top)
                    tot = tot + w
                    acc = acc + w * precv[g, zs, pl.ds(lq * dlen, dlen), at].astype(F32)
                att[g, pl.ds(lq * dlen, dlen), at] = (acc / tot).astype(BF16)
        if g < nch - 1:
            def early(i, carry):
                at = pl.ds(pl.multiple_of(i * otile, otile), otile)
                r = jnp.dot(
                    att[g], ow_v[pl.ds(g * cw, cw), at], preferred_element_type=F32
                )
                oacc[:, at] = r if g == 0 else oacc[:, at] + r
                return carry

            lax.fori_loop(0, width // otile, early, 0)

    piece = width // n_seq
    ptile = min(256, piece)

    def project_out(dest, put):
        def one(i, carry):
            src = pl.ds(pl.multiple_of(dest * piece + i * ptile, 128), ptile)
            at = pl.ds(pl.multiple_of(i * ptile, ptile), ptile)
            r = jnp.dot(
                att[nch - 1], ow_v[pl.ds((nch - 1) * cw, cw), src], preferred_element_type=F32
            )
            put(at, src, oacc[:, src] + r if nch > 1 else r)
            return carry

        lax.fori_loop(0, piece // ptile, one, 0)

    order = list(range(1, nx)) + [0]
    for dx in order:
        def put_send(at, src, r):
            rsend[dx, :, at] = r.astype(BF16)

        project_out(seq_of(dx, 1 - c), put_send)
        cp = pltpu.make_async_remote_copy(
            src_ref=rsend.at[dx], dst_ref=rpart.at[dx], send_sem=d_send.at[dx],
            recv_sem=d_recv.at[dx], device_id={"seq": partner},
        )
        cp.start()
        pending.append(cp)

    def wait_part(dx):
        pltpu.make_async_remote_copy(
            src_ref=rsend.at[dx], dst_ref=rpart.at[dx], send_sem=d_send.at[dx],
            recv_sem=d_recv.at[dx], device_id={"seq": partner},
        ).wait_recv()

    for dx in order:
        def put_sum(at, src, r):
            rown[:, at] = r

        project_out(seq_of(dx, c), put_sum)
        wait_part(dx)
        if dx:
            rsend[nx + dx] = (rown[...] + rpart[dx].astype(F32)).astype(BF16)
            cp = pltpu.make_async_remote_copy(
                src_ref=rsend.at[nx + dx], dst_ref=rx.at[x], send_sem=r_send.at[dx],
                recv_sem=r_recv.at[x], device_id={"seq": seq_of(dx, c)},
            )
            cp.start()
            pending.append(cp)
        else:
            mine = pl.ds(pl.multiple_of(me * piece, 128), piece)
            rown[...] = rown[...] + rpart[0].astype(F32) + dec_states[:, mine].astype(F32)
    total = rown[...]
    for dx in range(1, nx):
        xs = lax.rem(x + dx, nx)
        pltpu.make_async_remote_copy(
            src_ref=rsend.at[0], dst_ref=rx.at[xs], send_sem=r_send.at[0],
            recv_sem=r_recv.at[xs], device_id={"seq": xs * 2 + c},
        ).wait_recv()
        total = total + rx[xs].astype(F32)
    out[...] = total.astype(BF16)
    for cp in pending:
        cp.wait_send()


def body(
    states, enc_gain, dec_states, dec_gain, query_weight, key_value_weight, out_weight, question_of
):
    nz = lax.axis_size("qset")
    n_seq = lax.axis_size("seq")
    nx = n_seq // 2
    plen, width = states.shape[2], states.shape[3]
    nlq, dlen = dec_states.shape[0], dec_states.shape[1]
    cols = query_weight.shape[1]
    rows = nlq * dlen
    piece = width // n_seq
    npairs = cols // 128
    nch = 4 if npairs % 4 == 0 else npairs
    cw = cols // nch
    cfg = (n_seq, nz, nlq, plen, dlen, width, cols)
    any_spec = pl.BlockSpec(memory_space=pl.ANY)
    vmem = pl.BlockSpec(memory_space=pltpu.VMEM)
    dma = pltpu.SemaphoreType.DMA
    result = pl.pallas_call(
        functools.partial(kernel, cfg),
        out_shape=jax.ShapeDtypeStruct((rows, piece), BF16),
        in_specs=[pl.BlockSpec(memory_space=pltpu.SMEM), any_spec, vmem, vmem, vmem,
                  any_spec, any_spec, any_spec],
        out_specs=vmem,
        scratch_shapes=[
            pltpu.VMEM((n_seq, plen, width), BF16),
            pltpu.VMEM((width, cols), BF16),
            pltpu.VMEM((2, width, 2, 128), BF16),
            pltpu.VMEM((1024, 128), F32),
            pltpu.VMEM((width, 2 * cols), BF16),
            pltpu.VMEM((cols, width), BF16),
            pltpu.VMEM((2 * plen, width), BF16),
            pltpu.VMEM((nx, 2 * plen, 2 * cols), BF16),
            pltpu.VMEM((nlq * nz, dlen, cols), BF16),
            pltpu.VMEM((n_seq, dlen, cw), F32),
            pltpu.VMEM((n_seq, dlen, cw), F32),
            pltpu.VMEM((nch, nz, rows, cw), BF16),
            pltpu.VMEM((nch, nz, 8, 128), F32),
            pltpu.VMEM((nch, nz, rows, cw), BF16),
            pltpu.VMEM((nch, nz, 8, 128), F32),
            pltpu.VMEM((nch, rows, cw), BF16),
            pltpu.VMEM((rows, width), F32),
            pltpu.VMEM((2 * nx, rows, piece), BF16),
            pltpu.VMEM((nx, rows, piece), BF16),
            pltpu.VMEM((nx, rows, piece), BF16),
            pltpu.VMEM((rows, piece), F32),
            dma((4,)), dma((2,)),
            dma((2, nx, CHUNKS)), dma((n_seq, CHUNKS)),
            dma((nz,)), dma((nz,)),
            dma((nch, nz)), dma((nch, nz)), dma((nch, nz)), dma((nch, nz)),
            dma((nx,)), dma((nx,)), dma((nx,)), dma((nx,)),
        ],
        compiler_params=pltpu.CompilerParams(
            collective_id=0, has_side_effects=True, vmem_limit_bytes=63 * 1024 * 1024
        ),
        name="reader",
    )(
        question_of[:, :, 0], states.reshape(plen, width), enc_gain,
        dec_states.reshape(rows, width), dec_gain,
        query_weight, key_value_weight, out_weight,
    )
    return result.reshape(nlq, dlen, piece)


def solution(mesh):
    return jax.shard_map(
        body,
        mesh=mesh,
        in_specs=(
            P(("groups", "qset"), "seq", None, None),
            P(),
            P(("groups", "qset"), None, None),
            P(),
            P(None, "seq"),
            P(None, None, "seq"),
            P("seq", None),
            P("groups", None, None),
        ),
        out_specs=P(("groups", "qset"), None, "seq"),
        check_vma=False,
    )
```

profile of v0, /device:TPU:0, one launch (start us, length us, event | category | flops | bytes accessed | tf_op | source)
XLA Modules:
  0.0 91.0 jit_solution(5504013119977543398)
XLA Ops:
  0.0 89.3 %reader.1 = bf16[128,1024]{1,0:T(8,128)(2,1)} custom-call(s32[4,4]{1,0:T(4,128)} %bitcast.7, bf16[128,4096]{1,0:T(8,128)(2,1)} %bitcast.5, bf16[4096]{0:T(1024)(128)(2,1)} %enc_gain.1, bf16[128,4096]{1,0:T(8,128)(2,1)} %bitcast.6, bf16[4096]{0:T(1024)(128)(2,1)} %dec_gain.1, bf16[4096,1024]{1,0:T(8,128)(2,1)} %qw.1, bf16[4096,2,1024]{2,1,0:T(2,128)(2,1)} %kvw.1, ...), custom_call_target="tpu_custom_call" | custom-call | tf_op jit(solution)/shard_map/reader/pallas_call | solution.py:395
  89.3 1.7 %copy.10 = bf16[2,64,1024]{2,1,0:T(8,128)(2,1)} copy(bf16[2,64,1024]{2,1,0:T(8,128)(2,1)} %bitcast.4) | data formatting | bytes 524288
where the time goes:
time: 91.2 us; the launch traced here: 91 us
  Pallas kernels  89.3 us (98%)
  local copies, waits for them, and re-layouts  1.67 us (2%)
    pallas_call x1, Pallas kernels, body(): pl.pallas_call(functools.partial(kernel, cfg), out_shape=jax.ShapeDtypeSt...  89.3 us

commit v1 on v0

v1 whole, which is shorter than its diff:
```python
import functools
import jax
import jax.numpy as jnp
from jax import lax
from jax.experimental import pallas as pl
from jax.experimental.pallas import tpu as pltpu
from jax.sharding import PartitionSpec as P

HD = 64
EPSILON = 1e-06
DEAD = -1e30
CH = 2
F32 = jnp.float32
BF16 = jnp.bfloat16
scope = jax.named_scope


def norm_rows(load, store, gain, rows):
    step = 16

    def one(i, carry):
        at = pl.multiple_of(i * step, step)
        x = load(at, step).astype(F32)
        ms = jnp.mean(x * x, axis=-1, keepdims=True)
        store(at, step, (x * lax.rsqrt(ms + EPSILON) * gain).astype(BF16))
        return carry

    lax.fori_loop(0, rows // step, one, 0, unroll=2)


def kernel(
    cfg, qo, states, enc_gain, dec_states, dec_gain, qw, kvw, ow, out,
    xin, dec_v, gat, qw_v, raw, pulled, kv_v, ow_v, xn, kvs, qall, a_s, e_s,
    ps, es, pr, er, att, dsend, dpart, xsend, rx, rown,
    local_sem, raw_sem, ow_sem, xp_send, xs_send, xf_send, xs_recv, q_send, q_recv,
    ps_send, es_send, pr_recv, er_recv, d_send, d_recv, r_send, r_recv,
):
    n_seq, nz, nlq, plen, dlen, width, cols = cfg
    nx = n_seq // 2
    npairs = cols // 128
    rows = nlq * dlen
    hr = plen // 2
    cr = hr // CH
    piece = width // n_seq
    me = lax.axis_index("seq")
    z = lax.axis_index("qset")
    x = me // 2
    c = lax.rem(me, 2)
    partner = x * 2 + (1 - c)
    up_ok = z < nz - 1
    down_ok = z > 0

    def seq_of(dx, core):
        return lax.rem(x + dx, nx) * 2 + core

    barrier = pltpu.get_barrier_semaphore()
    for dx in range(1, nx):
        pl.semaphore_signal(barrier, 1, device_id={"seq": seq_of(dx, c)})
    pl.semaphore_signal(barrier, 1, device_id={"seq": partner})

    @pl.when(up_ok)
    def _():
        pl.semaphore_signal(barrier, 1, device_id={"qset": z + 1})

    @pl.when(down_ok)
    def _():
        pl.semaphore_signal(barrier, 1, device_id={"qset": z - 1})

    own_copy = pltpu.make_async_copy(states, xin, local_sem.at[0])
    own_copy.start()
    dec_copy = pltpu.make_async_copy(dec_states, dec_v, local_sem.at[1])
    dec_copy.start()
    qw_copy = pltpu.make_async_copy(qw, qw_v, local_sem.at[2])
    qw_copy.start()
    nblocks = cols // 128
    slots = raw.shape[0]
    kv2 = kvw.reshape(2 * width, cols)

    def raw_copy(b):
        return pltpu.make_async_copy(
            kv2.at[:, pl.ds(b * 128, 128)], raw.at[b % slots], raw_sem.at[b % slots]
        )

    def ow_copy(b):
        i, h2, k = b // 4, (b // 2) % 2, b % 2
        src = (2 * i + k) * 128 + h2 * HD
        return pltpu.make_async_copy(
            ow.at[pl.ds(src, HD)], ow_v.at[pl.ds(b * HD, HD)], ow_sem.at[b]
        )

    eg = enc_gain[...].astype(F32).reshape(1, width)
    dg = dec_gain[...].astype(F32).reshape(1, width)
    own_copy.wait()
    for b in range(min(slots, nblocks)):
        raw_copy(b).start()

    def put_own(at, n, v):
        gat[me, pl.ds(at, n), :] = v

    with scope("own_norm"):
        norm_rows(lambda at, n: xin[pl.ds(at, n), :], put_own, eg, plen)
    with scope("barrier"):
        pl.semaphore_wait(
            barrier, nx - 1 + 1 + up_ok.astype(jnp.int32) + down_ok.astype(jnp.int32)
        )

    def state_copy(slot, half, ch, to, send_sem):
        part = gat.at[slot, pl.ds(pl.multiple_of(half * hr + ch * cr, cr), cr)]
        return pltpu.make_async_remote_copy(
            src_ref=part, dst_ref=part, send_sem=send_sem,
            recv_sem=xs_recv.at[slot, half * CH + ch], device_id={"seq": to},
        )

    def wait_state(slot, half, ch):
        state_copy(slot, half, ch, partner, xp_send.at[0, 0]).wait_recv()

    def to_partner(first, ch):
        half = 1 - c if first else c
        return state_copy(me, half, ch, partner, xp_send.at[0 if first else 1, ch])

    def over_x(k, dx, ch):
        return state_copy(x * 2 + k, c, ch, seq_of(dx, c), xs_send.at[k, dx, ch])

    def start_over_x(k):
        for ch in range(CH):
            for dx in range(1, nx):
                over_x(k, dx, ch).start()

    def passed_on(k, dx, ch):
        return state_copy(seq_of(dx, k), c, ch, partner, xf_send.at[k, dx, ch])

    def forward(k, ch):
        for dx in range(1, nx):
            wait_state(seq_of(dx, k), c, ch)
            passed_on(k, dx, ch).start()

    for ch in range(CH):
        to_partner(True, ch).start()

    @pl.when(c == 0)
    def _():
        start_over_x(0)

    for ch in range(CH):
        to_partner(False, ch).start()

    def put_xn(at, n, v):
        xn[pl.ds(at, n), :] = v

    with scope("dec_norm"):
        dec_copy.wait()
        norm_rows(lambda at, n: dec_v[pl.ds(at, n), :], put_xn, dg, rows)

    with scope("x_start"):
        for ch in range(CH):
            wait_state(partner, c, ch)

        @pl.when(c == 1)
        def _():
            start_over_x(0)

        start_over_x(1)

    def q_copy(up, question):
        part = qall.at[question]
        return pltpu.make_async_remote_copy(
            src_ref=part, dst_ref=part, send_sem=q_send.at[0 if up else 1, question],
            recv_sem=q_recv.at[question], device_id={"qset": z + 1 if up else z - 1},
        )

    tile = min(256, cols)
    with scope("qproj"):
        qw_copy.wait()

        def q_tile(i, carry):
            at = pl.ds(pl.multiple_of(i * tile, tile), tile)
            r = jnp.dot(xn[...], qw_v[:, at], preferred_element_type=F32).astype(BF16)
            for lq in range(nlq):
                qall[z * nlq + lq, :, at] = r[lq * dlen:(lq + 1) * dlen]
            return carry

        lax.fori_loop(0, cols // tile, q_tile, 0, unroll=2)
    for lq in range(nlq):
        @pl.when(up_ok)
        def _():
            q_copy(True, z * nlq + lq).start()

        @pl.when(down_ok)
        def _():
            q_copy(False, z * nlq + lq).start()

    def pass_q(j, lq):
        @pl.when((z - j >= 0) & up_ok)
        def _():
            q_copy(True, (z - j) * nlq + lq).wait_recv()
            q_copy(True, (z - j) * nlq + lq).start()

        @pl.when((z + j < nz) & down_ok)
        def _():
            q_copy(False, (z + j) * nlq + lq).wait_recv()
            q_copy(False, (z + j) * nlq + lq).start()

    step = 256

    def pull_block(b):
        raw_copy(b).wait()
        flat = raw.at[b % slots]

        def pull(i, carry):
            for u in range(4):
                s = i * 4 + u
                buf = pulled.at[pl.ds(u * step, step)]
                buf[...] = flat[pl.ds(pl.multiple_of(s * step, step), step), :].astype(F32)
                at = pl.ds(pl.multiple_of(s * (step // 2), step // 2), step // 2)
                kv_v[at, pl.ds(b * 128, 128)] = buf[pl.ds(0, step // 2, stride=2), :].astype(BF16)
                kv_v[at, pl.ds(cols + b * 128, 128)] = (
                    buf[pl.ds(1, step // 2, stride=2), :].astype(BF16)
                )
            return carry

        lax.fori_loop(0, 2 * width // step // 4, pull, 0)
        if b + slots < nblocks:
            raw_copy(b + slots).start()

    with scope("pull"):
        for b in range(nblocks):
            pull_block(b)
            if b == (nblocks + 1) // 2 and nz > 2:
                pass_q(1, 0)
    for b in range(cols // HD):
        ow_copy(b).start()

    flat_gat = gat.reshape(n_seq * plen, width)
    flat_kvs = kvs.reshape(n_seq * plen, 2 * cols)
    ktile = min(256, cols)

    def project(first, count, lo, hi):
        base = pl.multiple_of(first * plen, plen)

        def kv_tile(i, carry):
            at = pl.ds(pl.multiple_of(i * ktile, ktile), ktile)
            r = jnp.dot(
                flat_gat[pl.ds(base, count * plen), :], kv_v[:, at],
                preferred_element_type=F32,
            )
            flat_kvs[pl.ds(base, count * plen), at] = r.astype(BF16)
            return carry

        lax.fori_loop(lo * cols // ktile, hi * cols // ktile, kv_tile, 0, unroll=2)

    with scope("fwd0"):
        forward(0, 0)
    with scope("q_fwd0"):
        if nz > 2:
            for lq in range(1, nlq):
                pass_q(1, lq)
        for ch in range(CH):
            wait_state(partner, 1 - c, ch)
    with scope("proj_own0"):
        project(x * 2, 2, 0, 1)
    with scope("q_fwd1"):
        if nz > 3:
            pass_q(2, 0)
    with scope("proj_own1"):
        project(x * 2, 2, 1, 2)
    with scope("fwd1"):
        if nz > 3:
            for lq in range(1, nlq):
                pass_q(2, lq)
        forward(0, 1)
        for ch in range(CH):
            for dx in range(1, nx):
                wait_state(seq_of(dx, 0), 1 - c, ch)
    with scope("proj_a"):
        for dx in range(1, nx):
            project(seq_of(dx, 0), 1, 0, 2)
    with scope("q_fwd2"):
        for j in range(3, nz - 1):
            for lq in range(nlq):
                pass_q(j, lq)
    with scope("fwd2"):
        forward(1, 0)

    low = lax.broadcasted_iota(jnp.int32, (dlen, 128), 1) < HD

    def attend(p, j):
        at = pl.ds(pl.multiple_of(j * 128, 128), 128)
        vat = pl.ds(pl.multiple_of(cols + j * 128, 128), 128)
        q = qall[qo[z, p], :, at]
        zero = jnp.zeros_like(q)
        q2 = jnp.concatenate([jnp.where(low, q, zero), jnp.where(low, zero, q)], axis=0)
        s = lax.dot_general(
            kvs[p, :, at], q2, (((1,), (1,)), ((), ())), preferred_element_type=F32
        )
        m = jnp.max(s, axis=0, keepdims=True)
        w = jnp.exp(s - m)
        l = jnp.sum(w, axis=0, keepdims=True)
        o = lax.dot_general(
            kvs[p, :, vat], w.astype(BF16), (((0,), (0,)), ((), ())),
            preferred_element_type=F32,
        )
        a = jnp.where(low, o[:HD], o[HD:]) * (1.0 / l)
        a_s[p, pl.ds(pl.multiple_of(j * HD, HD), HD), :] = a
        e_s[p, pl.ds(j, 1), :] = m + jnp.log(l)

    def attend_all(ps_list):
        for p in ps_list:
            lax.fori_loop(0, npairs, lambda j, carry, p=p: (attend(p, j), carry)[1], 0, unroll=8 if npairs % 8 == 0 else 1)

    if npairs < 8:
        e_s[...] = jnp.zeros(e_s.shape, F32)
    with scope("wait_q"):
        for question in range(nlq * nz):
            b = question // nlq

            @pl.when(((b < z) & (z == nz - 1)) | ((b > z) & (z == 0)))
            def _():
                q_copy(True, question).wait_recv()
    with scope("attend_own"):
        attend_all([x * 2, x * 2 + 1])
    with scope("attend_a"):
        attend_all([seq_of(dx, 0) for dx in range(1, nx)])

    @pl.when(z == 0)
    def _():
        er[0] = jnp.full(er.shape[1:], DEAD, F32)
        pr[0] = jnp.zeros(pr.shape[1:], BF16)

    @pl.when(z == nz - 1)
    def _():
        er[1] = jnp.full(er.shape[1:], DEAD, F32)
        pr[1] = jnp.zeros(pr.shape[1:], BF16)

    with scope("fwd3"):
        forward(1, 1)
        for ch in range(CH):
            for dx in range(1, nx):
                wait_state(seq_of(dx, 1), 1 - c, ch)
    with scope("proj_b"):
        for dx in range(1, nx):
            project(seq_of(dx, 1), 1, 0, 2)
    with scope("attend_b"):
        attend_all([seq_of(dx, 1) for dx in range(1, nx)])

    def terms(question, others):
        first = jnp.int32(0)
        second = jnp.int32(0)
        count = jnp.int32(0)
        for p in range(n_seq):
            hit = qo[z, p] == question
            first = jnp.where(hit & (count == 0), p, first)
            second = jnp.where(hit & (count == 1), p, second)
            count = count + hit.astype(jnp.int32)
        e = [jnp.where(count >= 1, e_s[first], DEAD), jnp.where(count >= 2, e_s[second], DEAD)]
        e += [er[d, question] for d in others]
        top = functools.reduce(jnp.maximum, e)
        w = [jnp.exp(t - top) for t in e]
        tot = functools.reduce(jnp.add, w)
        inv = 1.0 / tot
        w = [t * inv for t in w]

        def block(j):
            at = pl.ds(j * HD, HD)
            parts = [a_s[first, at, :], a_s[second, at, :]]
            parts += [pr[d, question, at, :].astype(F32) for d in others]
            return functools.reduce(
                jnp.add, [t * u[j:j + 1, :] for t, u in zip(parts, w, strict=True)]
            )

        return block, top + jnp.log(tot)

    def result_copies(d, question):
        to = z + 1 - 2 * d
        return [
            pltpu.make_async_remote_copy(
                src_ref=src.at[d, question], dst_ref=dst.at[d, question],
                send_sem=ss.at[d, question], recv_sem=rs.at[d, question],
                device_id={"qset": to},
            )
            for src, dst, ss, rs in ((es, er, es_send, er_recv), (ps, pr, ps_send, pr_recv))
        ]

    def sends(d, dest):
        return jnp.where(d == 0, dest > z, dest < z)

    def hop(d, k, lq):
        dest = jnp.where(d == 0, nz - 1 - k, k)
        question = dest * nlq + lq

        @pl.when(sends(d, dest))
        def _():
            @pl.when(jnp.where(d == 0, z > 0, z < nz - 1))
            def _():
                for cp in result_copies(d, question):
                    cp.wait_recv()

            block, e = terms(question, [d])
            for j in range(npairs):
                ps[d, question, pl.ds(j * HD, HD), :] = block(j).astype(BF16)
            es[d, question] = e
            for cp in result_copies(d, question):
                cp.start()

    near = (2 * z >= nz).astype(jnp.int32)
    with scope("chain"):
        for k in range(nz - 1):
            for d in (near, 1 - near):
                for lq in range(nlq):
                    hop(d, k, lq)

    ptile = min(512, piece)
    order = list(range(1, nx)) + [0]

    def project_out(lq, dest, put):
        for i in range(piece // ptile):
            src = pl.ds(pl.multiple_of(dest * piece + i * ptile, 128), ptile)
            put(pl.ds(i * ptile, ptile), jnp.dot(att[lq], ow_v[:, src], preferred_element_type=F32))

    def d_copy(lq, dx):
        return pltpu.make_async_remote_copy(
            src_ref=dsend.at[lq, dx], dst_ref=dpart.at[lq, dx], send_sem=d_send.at[lq, dx],
            recv_sem=d_recv.at[lq, dx], device_id={"seq": partner},
        )

    def r_copy(lq, dx):
        return pltpu.make_async_remote_copy(
            src_ref=xsend.at[lq, dx], dst_ref=rx.at[lq, x], send_sem=r_send.at[lq, dx],
            recv_sem=r_recv.at[lq, x], device_id={"seq": seq_of(dx, c)},
        )

    for lq in range(nlq):
        question = z * nlq + lq
        with scope("wait_res"):
            for d in range(2):
                @pl.when(z > 0 if d == 0 else z < nz - 1)
                def _():
                    for cp in result_copies(d, question):
                        cp.wait_recv()
        with scope("finish"):
            block, _ = terms(question, [0, 1])
            for i in range(npairs // 2):
                t = jnp.transpose(jnp.concatenate([block(2 * i), block(2 * i + 1)], axis=0))
                t = t.astype(BF16)
                att[lq, :, pl.ds(2 * i * 128, 128)] = t[:HD]
                att[lq, :, pl.ds((2 * i + 1) * 128, 128)] = t[HD:]
            if lq == 0:
                for b in range(cols // HD):
                    ow_copy(b).wait()
        with scope("out"):
            for dx in order:
                def put_send(at, r):
                    dsend[lq, dx, :, at] = r.astype(BF16)

                project_out(lq, seq_of(dx, 1 - c), put_send)
                d_copy(lq, dx).start()
            for dx in order:
                def put_sum(at, r):
                    rown[lq, dx, :, at] = r

                project_out(lq, seq_of(dx, c), put_sum)
        with scope("pair_sum"):
            for dx in order:
                d_copy(lq, dx).wait_recv()
                both = rown[lq, dx] + dpart[lq, dx].astype(F32)
                if dx:
                    xsend[lq, dx] = both.astype(BF16)
                    r_copy(lq, dx).start()
                else:
                    mine = pl.ds(pl.multiple_of(me * piece, 128), piece)
                    rown[lq, 0] = both + dec_v[pl.ds(lq * dlen, dlen), mine].astype(F32)
    for lq in range(nlq):
        with scope("final"):
            total = rown[lq, 0]
            for dx in range(1, nx):
                xs = lax.rem(x + dx, nx)
                pltpu.make_async_remote_copy(
                    src_ref=xsend.at[lq, 0], dst_ref=rx.at[lq, xs], send_sem=r_send.at[lq, 0],
                    recv_sem=r_recv.at[lq, xs], device_id={"seq": xs * 2 + c},
                ).wait_recv()
                total = total + rx[lq, xs].astype(F32)
            out[pl.ds(lq * dlen, dlen), :] = total.astype(BF16)

    for ch in range(CH):
        to_partner(True, ch).wait_send()
        to_partner(False, ch).wait_send()
        for k in range(2):
            for dx in range(1, nx):
                over_x(k, dx, ch).wait_send()
                passed_on(k, dx, ch).wait_send()
    for question in range(nlq * nz):
        b = question // nlq

        @pl.when(up_ok & (b <= z))
        def _():
            q_copy(True, question).wait_send()

        @pl.when(down_ok & (b >= z))
        def _():
            q_copy(False, question).wait_send()

        for d in range(2):
            @pl.when(sends(d, b))
            def _():
                for cp in result_copies(d, question):
                    cp.wait_send()
    for lq in range(nlq):
        for dx in range(nx):
            d_copy(lq, dx).wait_send()
            if dx:
                r_copy(lq, dx).wait_send()


def body(
    states, enc_gain, dec_states, dec_gain, query_weight, key_value_weight, out_weight, question_of
):
    nz = lax.axis_size("qset")
    n_seq = lax.axis_size("seq")
    nx = n_seq // 2
    plen, width = states.shape[2], states.shape[3]
    nlq, dlen = dec_states.shape[0], dec_states.shape[1]
    cols = query_weight.shape[1]
    rows = nlq * dlen
    piece = width // n_seq
    half = cols // 2
    nq = nlq * nz
    slots = min(4, cols // 128)
    cfg = (n_seq, nz, nlq, plen, dlen, width, cols)
    any_spec = pl.BlockSpec(memory_space=pl.ANY)
    vmem = pl.BlockSpec(memory_space=pltpu.VMEM)
    dma = pltpu.SemaphoreType.DMA
    result = pl.pallas_call(
        functools.partial(kernel, cfg),
        out_shape=jax.ShapeDtypeStruct((rows, piece), BF16),
        in_specs=[pl.BlockSpec(memory_space=pltpu.SMEM), any_spec, vmem, any_spec, vmem,
                  any_spec, any_spec, any_spec],
        out_specs=vmem,
        scratch_shapes=[
            pltpu.VMEM((plen, width), BF16),
            pltpu.VMEM((rows, width), BF16),
            pltpu.VMEM((n_seq, plen, width), BF16),
            pltpu.VMEM((width, cols), BF16),
            pltpu.VMEM((slots, 2 * width, 128), BF16),
            pltpu.VMEM((1024, 128), F32),
            pltpu.VMEM((width, 2 * cols), BF16),
            pltpu.VMEM((cols, width), BF16),
            pltpu.VMEM((rows, width), BF16),
            pltpu.VMEM((n_seq, plen, 2 * cols), BF16),
            pltpu.VMEM((nq, dlen, cols), BF16),
            pltpu.VMEM((n_seq, half, 128), F32),
            pltpu.VMEM((n_seq, 8, 128), F32),
            pltpu.VMEM((2, nq, half, 128), BF16),
            pltpu.VMEM((2, nq, 8, 128), F32),
            pltpu.VMEM((2, nq, half, 128), BF16),
            pltpu.VMEM((2, nq, 8, 128), F32),
            pltpu.VMEM((nlq, dlen, cols), BF16),
            pltpu.VMEM((nlq, nx, dlen, piece), BF16),
            pltpu.VMEM((nlq, nx, dlen, piece), BF16),
            pltpu.VMEM((nlq, nx, dlen, piece), BF16),
            pltpu.VMEM((nlq, nx, dlen, piece), BF16),
            pltpu.VMEM((nlq, nx, dlen, piece), F32),
            dma((3,)), dma((slots,)), dma((cols // HD,)),
            dma((2, CH)), dma((2, nx, CH)), dma((2, nx, CH)), dma((n_seq, 2 * CH)),
            dma((2, nq)), dma((nq,)),
            dma((2, nq)), dma((2, nq)), dma((2, nq)), dma((2, nq)),
            dma((nlq, nx)), dma((nlq, nx)), dma((nlq, nx)), dma((nlq, nx)),
        ],
        compiler_params=pltpu.CompilerParams(
            collective_id=0, has_side_effects=True, vmem_limit_bytes=63 * 1024 * 1024
        ),
        name="reader",
    )(
        question_of[:, :, 0], states.reshape(plen, width), enc_gain,
        dec_states.reshape(rows, width), dec_gain,
        query_weight, key_value_weight, out_weight,
    )
    return result.reshape(nlq, dlen, piece)


def solution(mesh):
    return jax.shard_map(
        body,
        mesh=mesh,
        in_specs=(
            P(("groups", "qset"), "seq", None, None),
            P(),
            P(("groups", "qset"), None, None),
            P(),
            P(None, "seq"),
            P(None, None, "seq"),
            P("seq", None),
            P("groups", None, None),
        ),
        out_specs=P(("groups", "qset"), None, "seq"),
        check_vma=False,
    )
```

time: 91.2 us -> 68.3 us (0.75)
  Pallas kernels: 89.3 us -> 65.7 us
    pallas_call x1, Pallas kernels: 89.3 us -> 65.7 us  [body(): pl.pallas_call(functools.partial(kernel, cfg), out_shape=jax.ShapeDtypeSt...]
where the time goes in v1:
time: 68.3 us; the launch traced here: 67.4 us
  Pallas kernels  65.7 us (96%)
  local copies, waits for them, and re-layouts  1.67 us (2%)
    pallas_call x1, Pallas kernels, body(): pl.pallas_call(functools.partial(kernel, cfg), out_shape=jax.ShapeDtypeSt...  65.7 us
    unnamed x1, local copies, waits for them, and re-layouts  1.67 us

profile of v1, /device:TPU:0, one launch (start us, length us, event | category | flops | bytes accessed | tf_op | source)
XLA Modules:
  0.0 67.4 jit_solution(7647975335258887826)
XLA Ops:
  0.0 65.7 %reader.1 = bf16[128,1024]{1,0:T(8,128)(2,1)} custom-call(s32[4,4]{1,0:T(4,128)} %bitcast.7, bf16[128,4096]{1,0:T(8,128)(2,1)} %bitcast.5, bf16[4096]{0:T(1024)(128)(2,1)} %enc_gain.1, bf16[128,4096]{1,0:T(8,128)(2,1)} %bitcast.6, bf16[4096]{0:T(1024)(128)(2,1)} %dec_gain.1, bf16[4096,1024]{1,0:T(8,128)(2,1)} %qw.1, bf16[4096,2,1024]{2,1,0:T(2,128)(2,1)} %kvw.1, ...), custom_call_target="tpu_custom_call" | custom-call | tf_op jit(solution)/shard_map/reader/pallas_call | solution.py:531
  65.7 1.7 %copy.10 = bf16[2,64,1024]{2,1,0:T(8,128)(2,1)} copy(bf16[2,64,1024]{2,1,0:T(8,128)(2,1)} %bitcast.4) | data formatting | bytes 524288

commit v2 on v1

v2 whole, which is shorter than its diff:
```python
import functools
import jax
import jax.numpy as jnp
from jax import lax
from jax.experimental import pallas as pl
from jax.experimental.pallas import tpu as pltpu
from jax.sharding import PartitionSpec as P

HD = 64
EPSILON = 1e-06
DEAD = -1e30
CHUNKS = (2, 4)
KT = 1024
F32 = jnp.float32
BF16 = jnp.bfloat16
scope = jax.named_scope


def norm_rows(load, store, gain, rows):
    step = 16

    def one(i, carry):
        at = pl.multiple_of(i * step, step)
        x = load(at, step).astype(F32)
        ms = jnp.mean(x * x, axis=-1, keepdims=True)
        store(at, step, (x * lax.rsqrt(ms + EPSILON) * gain).astype(BF16))
        return carry

    lax.fori_loop(0, rows // step, one, 0, unroll=2)


def kernel(
    cfg, qo, states, enc_gain, dec_states, dec_gain, qw, kvw, ow, out,
    eg_v, dg_v, xin, dec_v, gat, qw_v, raw, pulled, kv_v, ow_v, xn, kvs, qall, a_s, e_s,
    ps, pr, pick, att, dsend, dpart, xsend, rx, rown, s_buf, w_buf, i_buf, out_v, acc, pacc,
    local_sem, raw_sem, ow_sem, xp_send, xp_recv, xs_send, xf_send, x_recv, q_send, q_recv,
    ps_send, pr_recv, d_send, d_recv, r_send, r_recv, out_sem,
):
    n_seq, nz, nlq, plen, dlen, width, cols = cfg
    nx = n_seq // 2
    npairs = cols // 128
    rows = nlq * dlen
    hr = plen // 2
    srows = cols // 2
    parts = 2 if npairs % 4 == 0 else 1
    prows = srows // parts
    ppairs = npairs // parts
    beyond = nlq * (nz - 1)
    packed = min(n_seq, beyond)
    piece = width // n_seq
    me = lax.axis_index("seq")
    z = lax.axis_index("qset")
    x = me // 2
    c = lax.rem(me, 2)
    partner = x * 2 + (1 - c)
    up_ok = z < nz - 1
    down_ok = z > 0

    def seq_of(dx, core):
        return lax.rem(x + dx, nx) * 2 + core

    barrier = pltpu.get_barrier_semaphore()
    for dx in range(1, nx):
        pl.semaphore_signal(barrier, 1, device_id={"seq": seq_of(dx, c)})
    pl.semaphore_signal(barrier, 1, device_id={"seq": partner})

    @pl.when(up_ok)
    def _():
        pl.semaphore_signal(barrier, 1, device_id={"qset": z + 1})

    @pl.when(down_ok)
    def _():
        pl.semaphore_signal(barrier, 1, device_id={"qset": z - 1})

    eg_copy = pltpu.make_async_copy(enc_gain, eg_v, local_sem.at[0])
    eg_copy.start()

    def own_copy(half):
        at = pl.ds(half * hr, hr)
        return pltpu.make_async_copy(states.at[at], xin.at[at], local_sem.at[1 + half])

    own_copy(0).start()
    own_copy(1).start()
    dg_copy = pltpu.make_async_copy(dec_gain, dg_v, local_sem.at[3])
    dg_copy.start()
    dec_copy = pltpu.make_async_copy(dec_states, dec_v, local_sem.at[4])
    dec_copy.start()
    qw_copy = pltpu.make_async_copy(qw, qw_v, local_sem.at[5])
    qw_copy.start()
    nblocks = cols // 128
    slots = raw.shape[0]
    kv2 = kvw.reshape(2 * width, cols)

    def raw_copy(b):
        return pltpu.make_async_copy(
            kv2.at[:, pl.ds(b * 128, 128)], raw.at[b % slots], raw_sem.at[b % slots]
        )

    def ow_copy(b):
        i, h2, k = b // 4, (b // 2) % 2, b % 2
        src = (2 * i + k) * 128 + h2 * HD
        return pltpu.make_async_copy(
            ow.at[pl.ds(src, HD)], ow_v.at[pl.ds(b * HD, HD)], ow_sem.at[0]
        )

    eg_copy.wait()
    eg = eg_v[...].astype(F32).reshape(1, width)

    def norm_own(half):
        own_copy(half).wait()

        def put(at, n, v):
            gat[me, pl.ds(half * hr + at, n), :] = v

        norm_rows(lambda at, n: xin[pl.ds(half * hr + at, n), :], put, eg, hr)

    with scope("own_norm"):
        norm_own(0)
    for b in range(min(slots, nblocks)):
        raw_copy(b).start()
    with scope("barrier"):
        pl.semaphore_wait(
            barrier, nx - 1 + 1 + up_ok.astype(jnp.int32) + down_ok.astype(jnp.int32)
        )

    def half_rows(slot, half):
        return gat.at[slot, pl.ds(pl.multiple_of(half * hr, hr), hr)]

    def to_partner(half):
        part = half_rows(me, half)
        return pltpu.make_async_remote_copy(
            src_ref=part, dst_ref=part, send_sem=xp_send.at[half], recv_sem=xp_recv.at[half],
            device_id={"seq": partner},
        )

    def from_partner(half):
        part = half_rows(partner, half)
        return pltpu.make_async_remote_copy(
            src_ref=part, dst_ref=part, send_sem=xp_send.at[half], recv_sem=xp_recv.at[half],
            device_id={"seq": partner},
        )

    def x_copy(slot, half, k, ch, to, send_sem, source):
        wide = width // CHUNKS[k]
        part = gat.at[
            slot, pl.ds(pl.multiple_of(half * hr, hr), hr), pl.ds(ch * wide, wide)
        ]
        return pltpu.make_async_remote_copy(
            src_ref=part, dst_ref=part, send_sem=send_sem,
            recv_sem=x_recv.at[source, half, k * CHUNKS[0] + ch], device_id={"seq": to},
        )

    def over_x(k, dx, ch):
        return x_copy(
            x * 2 + k, c, k, ch, seq_of(dx, c), xs_send.at[dx - 1, k * CHUNKS[0] + ch],
            nx - 1 - dx,
        )

    def start_over_x(k):
        for ch in range(CHUNKS[k]):
            for dx in range(1, nx):
                over_x(k, dx, ch).start()

    def passed_on(k, dx, ch, half):
        return x_copy(
            seq_of(dx, k), half, k, ch, partner, xf_send.at[dx - 1, k * CHUNKS[0] + ch], dx - 1
        )

    def forward(k, ch):
        for dx in range(1, nx):
            passed_on(k, dx, ch, c).wait_recv()
            passed_on(k, dx, ch, c).start()

    def wait_other(k, ch):
        for dx in range(1, nx):
            passed_on(k, dx, ch, 1 - c).wait_recv()

    @pl.when(c == 0)
    def _():
        start_over_x(0)

    @pl.when(c == 1)
    def _():
        to_partner(0).start()

    with scope("own_norm"):
        norm_own(1)
    to_partner(1).start()

    @pl.when(c == 0)
    def _():
        to_partner(0).start()

    def put_xn(at, n, v):
        xn[pl.ds(at, n), :] = v

    with scope("dec_norm"):
        dg_copy.wait()
        dec_copy.wait()
        dg = dg_v[...].astype(F32).reshape(1, width)
        norm_rows(lambda at, n: dec_v[pl.ds(at, n), :], put_xn, dg, rows)

    with scope("x_start"):
        from_partner(c).wait_recv()

        @pl.when(c == 1)
        def _():
            start_over_x(0)

        start_over_x(1)

    def q_copy(up, question):
        part = qall.at[question]
        return pltpu.make_async_remote_copy(
            src_ref=part, dst_ref=part, send_sem=q_send.at[0 if up else 1, question],
            recv_sem=q_recv.at[question], device_id={"qset": z + 1 if up else z - 1},
        )

    tile = min(512, cols)
    with scope("qproj"):
        qw_copy.wait()

        def q_tile(i, carry):
            at = pl.ds(pl.multiple_of(i * tile, tile), tile)
            r = jnp.dot(xn[...], qw_v[:, at], preferred_element_type=F32).astype(BF16)
            for lq in range(nlq):
                qall[z * nlq + lq, :, at] = r[lq * dlen:(lq + 1) * dlen]
            return carry

        lax.fori_loop(0, cols // tile, q_tile, 0)
    for lq in range(nlq):
        @pl.when(up_ok)
        def _():
            q_copy(True, z * nlq + lq).start()

        @pl.when(down_ok)
        def _():
            q_copy(False, z * nlq + lq).start()

    def pass_q(j, lq):
        @pl.when((z - j >= 0) & up_ok)
        def _():
            q_copy(True, (z - j) * nlq + lq).wait_recv()
            q_copy(True, (z - j) * nlq + lq).start()

        @pl.when((z + j < nz) & down_ok)
        def _():
            q_copy(False, (z + j) * nlq + lq).wait_recv()
            q_copy(False, (z + j) * nlq + lq).start()

    step = 256

    def pull_block(b):
        raw_copy(b).wait()
        flat = raw.at[b % slots]

        def pull(i, carry):
            for u in range(4):
                s = i * 4 + u
                buf = pulled.at[pl.ds(u * step, step)]
                buf[...] = flat[pl.ds(pl.multiple_of(s * step, step), step), :].astype(F32)
                at = pl.ds(pl.multiple_of(s * (step // 2), step // 2), step // 2)
                kv_v[at, pl.ds(b * 128, 128)] = buf[pl.ds(0, step // 2, stride=2), :].astype(BF16)
                kv_v[at, pl.ds(cols + b * 128, 128)] = (
                    buf[pl.ds(1, step // 2, stride=2), :].astype(BF16)
                )
            return carry

        lax.fori_loop(0, 2 * width // step // 4, pull, 0)
        if b + slots < nblocks:
            raw_copy(b + slots).start()

    with scope("pull"):
        for b in range(nblocks):
            pull_block(b)
            if b == (nblocks + 1) // 2 and nz > 2:
                pass_q(1, 0)
    for b in range(cols // HD):
        ow_copy(b).start()

    flat_gat = gat.reshape(n_seq * plen, width)
    flat_kvs = kvs.reshape(n_seq * plen, 2 * cols)


    def project(first, count, lo, hi):
        base = pl.multiple_of(first * plen, plen)
        ktile = min(KT // count, cols)

        def kv_tile(i, carry):
            at = pl.ds(pl.multiple_of(i * ktile, ktile), ktile)
            r = jnp.dot(
                flat_gat[pl.ds(base, count * plen), :], kv_v[:, at],
                preferred_element_type=F32,
            )
            flat_kvs[pl.ds(base, count * plen), at] = r.astype(BF16)
            return carry

        lax.fori_loop(lo * cols // ktile, hi * cols // ktile, kv_tile, 0)

    with scope("fwd0"):
        forward(0, 0)
    with scope("q_fwd0"):
        if nz > 2:
            for lq in range(1, nlq):
                pass_q(1, lq)
        from_partner(1 - c).wait_recv()
    with scope("proj_own0"):
        project(x * 2, 2, 0, 1)
    with scope("q_fwd1"):
        if nz > 3:
            pass_q(2, 0)
    with scope("proj_own1"):
        project(x * 2, 2, 1, 2)
    with scope("fwd1"):
        if nz > 3:
            for lq in range(1, nlq):
                pass_q(2, lq)
        for ch in range(1, CHUNKS[0]):
            forward(0, ch)
        for ch in range(CHUNKS[0]):
            wait_other(0, ch)
    with scope("proj_a"):
        for dx in range(1, nx):
            project(seq_of(dx, 0), 1, 0, 2)
    with scope("q_fwd2"):
        for j in range(3, nz - 1):
            for lq in range(nlq):
                pass_q(j, lq)
    wide = width // CHUNKS[1]

    def project_part(dx, ch):
        p = seq_of(dx, 1)
        tile = min(KT, cols)
        for i in range(2 * cols // tile):
            at = pl.ds(i * tile, tile)
            r = jnp.dot(
                gat[p, :, pl.ds(ch * wide, wide)], kv_v[pl.ds(ch * wide, wide), at],
                preferred_element_type=F32,
            )
            if ch:
                r = r + acc[dx - 1, :, at]
            if ch < CHUNKS[1] - 1:
                acc[dx - 1, :, at] = r
            else:
                kvs[p, :, at] = r.astype(BF16)

    def take_part(ch):
        wait_other(1, ch)
        for dx in range(1, nx):
            project_part(dx, ch)

    with scope("b01"):
        forward(1, 0)
        forward(1, 1)
        take_part(0)
        take_part(1)
    with scope("b2"):
        forward(1, 2)
        take_part(2)

    low = lax.broadcasted_iota(jnp.int32, (dlen, 128), 1) < HD

    def attend_all(ps_list):
        units = [(u * npairs + j, p, j) for u, p in enumerate(ps_list) for j in range(npairs)]
        for n, p, j in units:
            q = qall[qo[z, p], :, pl.ds(j * 128, 128)]
            zero = jnp.zeros_like(q)
            q2 = jnp.concatenate([jnp.where(low, q, zero), jnp.where(low, zero, q)], axis=0)
            s_buf[n] = lax.dot_general(
                kvs[p, :, pl.ds(j * 128, 128)], q2, (((1,), (1,)), ((), ())),
                preferred_element_type=F32,
            )
        for n, p, j in units:
            s = s_buf[n]
            m = jnp.max(s, axis=0, keepdims=True)
            w = jnp.exp(s - m)
            l = jnp.sum(w, axis=0, keepdims=True)
            w_buf[n] = w.astype(BF16)
            i_buf[pl.ds(n, 1), :] = 1.0 / l
            e_s[p, pl.ds(j, 1), :] = m + jnp.log(l)
        for n, p, j in units:
            o = lax.dot_general(
                kvs[p, :, pl.ds(cols + j * 128, 128)], w_buf[n], (((0,), (0,)), ((), ())),
                preferred_element_type=F32,
            )
            a_s[p, pl.ds(j * HD, HD), :] = jnp.where(low, o[:HD], o[HD:]) * i_buf[n:n + 1, :]

    if npairs < 8:
        e_s[...] = jnp.zeros(e_s.shape, F32)
    with scope("wait_q"):
        for question in range(nlq * nz):
            b = question // nlq

            @pl.when(((b < z) & (z == nz - 1)) | ((b > z) & (z == 0)))
            def _():
                q_copy(True, question).wait_recv()
    with scope("fwd3"):
        forward(1, 3)
    with scope("attend_own"):
        attend_all([x * 2, x * 2 + 1])
    with scope("attend_a"):
        for dx in range(1, nx):
            attend_all([seq_of(dx, 0)])

    def put_logs(ref, e):
        hi = e.astype(BF16)
        rest = e - hi.astype(F32)
        mid = rest.astype(BF16)
        lo = (rest - mid.astype(F32)).astype(BF16)
        ref[pl.ds(prows, 16), :] = jnp.concatenate([hi, mid], axis=0)
        ref[pl.ds(prows + 16, 16), :] = jnp.concatenate([lo, jnp.zeros_like(lo)], axis=0)

    def get_logs(ref):
        two = ref[pl.ds(prows, 16), :].astype(F32)
        return two[:8] + two[8:] + ref[pl.ds(prows + 16, 16), :].astype(F32)[:8]

    with scope("b3"):
        take_part(3)
    with scope("attend_b"):
        for dx in range(1, nx):
            attend_all([seq_of(dx, 1)])

    near = (2 * z >= nz).astype(jnp.int32)
    sides = (near, 1 - near)

    def question_at(d, o):
        return jnp.where(d == 0, (nz - 1 - o // nlq) * nlq, o // nlq * nlq) + o % nlq

    def packing(d):
        edge = jnp.where(d == 0, 0, nz - 1)
        rank, ranks, found = jnp.int32(0), [], []
        for o in range(beyond):
            hit = jnp.int32(0)
            for p in range(n_seq):
                hit = hit | (qo[edge, p] == question_at(d, o)).astype(jnp.int32)
            ranks.append(jnp.minimum(rank, packed - 1))
            found.append(hit)
            rank = rank + hit
        return ranks, found

    plans = [packing(d) for d in sides]

    def terms(question, sources):
        first = jnp.int32(0)
        second = jnp.int32(0)
        count = jnp.int32(0)
        for p in range(n_seq):
            hit = qo[z, p] == question
            first = jnp.where(hit & (count == 0), p, first)
            second = jnp.where(hit & (count == 1), p, second)
            count = count + hit.astype(jnp.int32)
        e = [jnp.where(count >= 1, e_s[first], DEAD), jnp.where(count >= 2, e_s[second], DEAD)]
        e += [jnp.where(ok, get_logs(pick.at[side]), DEAD) for side, ok in sources]
        top = functools.reduce(jnp.maximum, e)
        w = [jnp.exp(t - top) for t in e]
        tot = functools.reduce(jnp.add, w)
        inv = 1.0 / tot
        w = [t * inv for t in w]

        def block(j):
            at = pl.ds(j * HD, HD)
            there = pl.ds(j * HD + (32 if j >= ppairs else 0), HD)
            values = [a_s[first, at, :], a_s[second, at, :]]
            values += [pick[side, there, :].astype(F32) for side, ok in sources]
            return functools.reduce(
                jnp.add, [t * u[j:j + 1, :] for t, u in zip(values, w, strict=True)]
            )

        return block, top + jnp.log(tot)

    def part_rows(h):
        return pl.ds(0, prows + 32) if h == 0 else pl.ds(prows + 32, prows)

    def result_copy(d, n, h):
        at = part_rows(h)
        return pltpu.make_async_remote_copy(
            src_ref=ps.at[d, n, at], dst_ref=pr.at[d, n, at], send_sem=ps_send.at[d, n, h],
            recv_sem=pr_recv.at[d, n, h], device_id={"qset": z + 1 - 2 * d},
        )

    def at_edge(d):
        return jnp.where(d == 0, z == 0, z == nz - 1)

    def after_edge(d):
        return jnp.where(d == 0, z == 1, z == nz - 2)

    def places(d):
        return jnp.where(d == 0, nz - 1 - z, z) * nlq

    def take(side, o, packed_o, h):
        d = sides[side]
        at = part_rows(h)
        ranks, _ = plans[side]

        @pl.when(after_edge(d))
        def _():
            if packed_o < packed:
                result_copy(d, packed_o, h).wait_recv()
            value = pr[d, 0, at, :]
            for n in range(1, min(packed_o, packed - 1) + 1):
                value = jnp.where(ranks[packed_o] == n, pr[d, n, at, :], value)
            pick[side, at, :] = value

        @pl.when(~(after_edge(d) | at_edge(d)))
        def _():
            result_copy(d, o, h).wait_recv()
            pick[side, at, :] = pr[d, o, at, :]

        @pl.when(at_edge(d))
        def _():
            pick[side, at, :] = jnp.zeros((at.size, 128), BF16)

    def have(side, packed_o):
        d = sides[side]
        _, found = plans[side]
        return ~at_edge(d) & (~after_edge(d) | (found[packed_o] > 0))

    def put_slot(d, n, block, e, h):
        for j in range(h * ppairs, (h + 1) * ppairs):
            ps[d, n, pl.ds(j * HD + (32 if h else 0), HD), :] = block(j).astype(BF16)
        if h == 0:
            put_logs(ps.at[d, n], e)
        result_copy(d, n, h).start()

    def first_hop(side):
        d = sides[side]
        ranks, found = plans[side]

        @pl.when(at_edge(d))
        def _():
            for n in range(packed):
                question = jnp.int32(-1)
                rank = jnp.int32(0)
                for o in range(beyond):
                    question = jnp.where((found[o] > 0) & (rank == n), question_at(d, o), question)
                    rank = rank + found[o]
                block, e = terms(question, [])
                for h in range(parts):
                    put_slot(d, n, block, e, h)

    def hop(side, o):
        d = sides[side]

        @pl.when((o < places(d)) & ~at_edge(d))
        def _():
            take(side, o, o, 0)
            block, e = terms(question_at(d, o), [(side, have(side, o))])
            put_slot(d, o, block, e, 0)
            for h in range(1, parts):
                take(side, o, o, h)
                put_slot(d, o, block, e, h)

    for question in range(nlq * nz):
        @pl.when(up_ok & (question // nlq <= z))
        def _():
            q_copy(True, question).wait_send()

        @pl.when(down_ok & (question // nlq >= z))
        def _():
            q_copy(False, question).wait_send()

    with scope("chain"):
        for side in range(2):
            first_hop(side)
        for k in range(nz - 1):
            for side in range(2):
                for lq in range(nlq):
                    hop(side, k * nlq + lq)

    for half in range(2):
        to_partner(half).wait_send()
    for k in range(2):
        for ch in range(CHUNKS[k]):
            for dx in range(1, nx):
                over_x(k, dx, ch).wait_send()
                passed_on(k, dx, ch, c).wait_send()

    order = list(range(1, nx)) + [0]

    def product(lq, dest, h):
        src = pl.ds(pl.multiple_of(dest * piece, piece), piece)
        heads = pl.ds(h * ppairs * 128, ppairs * 128)
        return jnp.dot(att[lq, :, heads], ow_v[heads, src], preferred_element_type=F32)

    def d_copy(lq, dx):
        return pltpu.make_async_remote_copy(
            src_ref=dsend.at[lq, dx], dst_ref=dpart.at[lq, dx], send_sem=d_send.at[lq, dx],
            recv_sem=d_recv.at[lq, dx], device_id={"seq": partner},
        )

    def r_copy(lq, dx):
        return pltpu.make_async_remote_copy(
            src_ref=xsend.at[lq, dx], dst_ref=rx.at[lq, x], send_sem=r_send.at[lq, dx - 1],
            recv_sem=r_recv.at[lq, nx - 1 - dx], device_id={"seq": seq_of(dx, c)},
        )

    for lq in range(nlq):
        def own_parts(h):
            with scope("wait_res"):
                last = beyond - nlq + lq
                for side in range(2):
                    take(side, places(sides[side]) + lq, last, h)
            with scope("finish"):
                block, _ = terms(z * nlq + lq, [(side, have(side, last)) for side in range(2)])
                for i in range(h * ppairs // 2, (h + 1) * ppairs // 2):
                    t = jnp.transpose(jnp.concatenate([block(2 * i), block(2 * i + 1)], axis=0))
                    t = t.astype(BF16)
                    att[lq, :, pl.ds(2 * i * 128, 128)] = t[:HD]
                    att[lq, :, pl.ds((2 * i + 1) * 128, 128)] = t[HD:]
                if lq == 0 and h == 0:
                    pltpu.make_async_copy(ow, ow_v, ow_sem.at[0]).wait()

        for h in range(parts - 1):
            own_parts(h)
            with scope("out_part"):
                for n in range(n_seq):
                    dest = seq_of(n // 2, (1 - c) if n % 2 == 0 else c)
                    pacc[n] = product(lq, dest, h)
        own_parts(parts - 1)

        def pair_sum(dx):
            d_copy(lq, dx).wait_recv()
            both = rown[lq, dx] + dpart[lq, dx].astype(F32)
            if dx:
                xsend[lq, dx] = both.astype(BF16)
                r_copy(lq, dx).start()
            else:
                mine = pl.ds(pl.multiple_of(me * piece, 128), piece)
                rown[lq, 0] = both + dec_v[pl.ds(lq * dlen, dlen), mine].astype(F32)

        with scope("out"):
            held = None
            for n, dx in enumerate(order):
                theirs = product(lq, seq_of(dx, 1 - c), parts - 1)
                if parts > 1:
                    theirs = theirs + pacc[2 * dx]
                if held is not None:
                    rown[lq, order[n - 1]] = held
                held = product(lq, seq_of(dx, c), parts - 1)
                if parts > 1:
                    held = held + pacc[2 * dx + 1]
                dsend[lq, dx] = theirs.astype(BF16)
                d_copy(lq, dx).start()
                if n > 1:
                    pair_sum(order[n - 2])
            rown[lq, order[-1]] = held
        with scope("pair_sum"):
            for dx in order[-2:]:
                pair_sum(dx)
    def out_copy(lq):
        return pltpu.make_async_copy(
            out_v.at[lq], out.at[pl.ds(lq * dlen, dlen)], out_sem.at[lq]
        )

    for d in range(2):
        for o in range(beyond):
            sent = (o < places(d)) & ((o < packed) | ~at_edge(d))

            @pl.when(sent)
            def _():
                for h in range(parts):
                    result_copy(d, o, h).wait_send()
    for lq in range(nlq):
        for dx in range(nx):
            d_copy(lq, dx).wait_send()
    for lq in range(nlq):
        with scope("final"):
            total = rown[lq, 0]
            for dx in range(1, nx):
                xs = lax.rem(x + dx, nx)
                pltpu.make_async_remote_copy(
                    src_ref=xsend.at[lq, 0], dst_ref=rx.at[lq, xs], send_sem=r_send.at[lq, 0],
                    recv_sem=r_recv.at[lq, dx - 1], device_id={"seq": xs * 2 + c},
                ).wait_recv()
                total = total + rx[lq, xs].astype(F32)
            out_v[lq] = total.astype(BF16)
            out_copy(lq).start()
    for lq in range(nlq):
        for dx in range(1, nx):
            r_copy(lq, dx).wait_send()
        out_copy(lq).wait()


def body(
    states, enc_gain, dec_states, dec_gain, query_weight, key_value_weight, out_weight, question_of
):
    nz = lax.axis_size("qset")
    n_seq = lax.axis_size("seq")
    nx = n_seq // 2
    plen, width = states.shape[2], states.shape[3]
    nlq, dlen = dec_states.shape[0], dec_states.shape[1]
    cols = query_weight.shape[1]
    rows = nlq * dlen
    piece = width // n_seq
    half = cols // 2
    nq = nlq * nz
    slots = min(3, cols // 128)
    nch = sum(CHUNKS)
    beyond = nlq * (nz - 1)
    parts = 2 if cols % 512 == 0 else 1
    cfg = (n_seq, nz, nlq, plen, dlen, width, cols)
    any_spec = pl.BlockSpec(memory_space=pl.ANY)
    dma = pltpu.SemaphoreType.DMA
    result = pl.pallas_call(
        functools.partial(kernel, cfg),
        out_shape=jax.ShapeDtypeStruct((rows, piece), BF16),
        in_specs=[pl.BlockSpec(memory_space=pltpu.SMEM), any_spec, any_spec, any_spec, any_spec,
                  any_spec, any_spec, any_spec],
        out_specs=any_spec,
        scratch_shapes=[
            pltpu.VMEM((width,), BF16),
            pltpu.VMEM((width,), BF16),
            pltpu.VMEM((plen, width), BF16),
            pltpu.VMEM((rows, width), BF16),
            pltpu.VMEM((n_seq, plen, width), BF16),
            pltpu.VMEM((width, cols), BF16),
            pltpu.VMEM((slots, 2 * width, 128), BF16),
            pltpu.VMEM((1024, 128), F32),
            pltpu.VMEM((width, 2 * cols), BF16),
            pltpu.VMEM((cols, width), BF16),
            pltpu.VMEM((rows, width), BF16),
            pltpu.VMEM((n_seq, plen, 2 * cols), BF16),
            pltpu.VMEM((nq, dlen, cols), BF16),
            pltpu.VMEM((n_seq, half, 128), F32),
            pltpu.VMEM((n_seq, 8, 128), F32),
            pltpu.VMEM((2, beyond, half + 32, 128), BF16),
            pltpu.VMEM((2, beyond, half + 32, 128), BF16),
            pltpu.VMEM((2, half + 32, 128), BF16),
            pltpu.VMEM((nlq, dlen, cols), BF16),
            pltpu.VMEM((nlq, nx, dlen, piece), BF16),
            pltpu.VMEM((nlq, nx, dlen, piece), BF16),
            pltpu.VMEM((nlq, nx, dlen, piece), BF16),
            pltpu.VMEM((nlq, nx, dlen, piece), BF16),
            pltpu.VMEM((nlq, nx, dlen, piece), F32),
            pltpu.VMEM((2 * cols // 128, plen, 128), F32),
            pltpu.VMEM((2 * cols // 128, plen, 128), BF16),
            pltpu.VMEM((max(8, 2 * cols // 128), 128), F32),
            pltpu.VMEM((nlq, dlen, piece), BF16),
            pltpu.VMEM((nx - 1, plen, 2 * cols), F32),
            pltpu.VMEM((n_seq, dlen, piece) if cols % 512 == 0 else (1, 8, 128), F32),
            dma((6,)), dma((slots,)), dma((1,)),
            dma((2,)), dma((2,)), dma((nx - 1, nch)), dma((nx - 1, nch)), dma((nx - 1, 2, nch)),
            dma((2, nq)), dma((nq,)), dma((2, beyond, parts)), dma((2, beyond, parts)),
            dma((nlq, nx)), dma((nlq, nx)), dma((nlq, nx - 1)), dma((nlq, nx - 1)), dma((nlq,)),
        ],
        compiler_params=pltpu.CompilerParams(
            collective_id=0, has_side_effects=True, vmem_limit_bytes=63 * 1024 * 1024
        ),
        name="reader",
    )(
        question_of[:, :, 0], states.reshape(plen, width), enc_gain,
        dec_states.reshape(rows, width), dec_gain,
        query_weight, key_value_weight, out_weight,
    )
    return result.reshape(nlq, dlen, piece)


def solution(mesh):
    return jax.shard_map(
        body,
        mesh=mesh,
        in_specs=(
            P(("groups", "qset"), "seq", None, None),
            P(),
            P(("groups", "qset"), None, None),
            P(),
            P(None, "seq"),
            P(None, None, "seq"),
            P("seq", None),
            P("groups", None, None),
        ),
        out_specs=P(("groups", "qset"), None, "seq"),
        check_vma=False,
    )
```

time: 68.3 us -> 60.5 us (0.89)
  the two profiles are of different devices: /device:TPU:0 before, /device:TPU:20 now
where the time goes in v2:
time: 60.5 us; the launch traced here: 60.3 us
  Pallas kernels  58.6 us (97%)
  local copies, waits for them, and re-layouts  1.67 us (3%)
    pallas_call x1, Pallas kernels, body(): pl.pallas_call(functools.partial(kernel, cfg), out_shape=jax.ShapeDtypeSt...  58.6 us
    unnamed x1, local copies, waits for them, and re-layouts  1.67 us

profile of v2, /device:TPU:20, one launch (start us, length us, event | category | flops | bytes accessed | tf_op | source)
XLA Modules:
  0.0 60.3 jit_solution(7575241448420727153)
XLA Ops:
  0.0 58.6 %reader.1 = bf16[128,1024]{1,0:T(8,128)(2,1)} custom-call(s32[4,4]{1,0:T(4,128)} %bitcast.7, bf16[128,4096]{1,0:T(8,128)(2,1)} %bitcast.5, bf16[4096]{0:T(1024)(128)(2,1)} %enc_gain.1, bf16[128,4096]{1,0:T(8,128)(2,1)} %bitcast.6, bf16[4096]{0:T(1024)(128)(2,1)} %dec_gain.1, bf16[4096,1024]{1,0:T(8,128)(2,1)} %qw.1, bf16[4096,2,1024]{2,1,0:T(2,128)(2,1)} %kvw.1, ...), custom_call_target="tpu_custom_call" | custom-call | tf_op jit(solution)/shard_map/reader/pallas_call | solution.py:704
  58.6 1.7 %copy.10 = bf16[2,64,1024]{2,1,0:T(8,128)(2,1)} copy(bf16[2,64,1024]{2,1,0:T(8,128)(2,1)} %bitcast.4) | data formatting | bytes 524288

commit v3 on v2

--- a/solution.py
+++ b/solution.py
@@ -32,9 +32,9 @@
 def kernel(
     cfg, qo, states, enc_gain, dec_states, dec_gain, qw, kvw, ow, out,
     eg_v, dg_v, xin, dec_v, gat, qw_v, raw, pulled, kv_v, ow_v, xn, kvs, qall, a_s, e_s,
-    ps, pr, pick, att, dsend, dpart, xsend, rx, rown, s_buf, w_buf, i_buf, out_v, acc, pacc,
+    ps, pr, pick, att, dsend, dpart, xsend, rx, rown, s_buf, w_buf, i_buf, acc, pacc,
     local_sem, raw_sem, ow_sem, xp_send, xp_recv, xs_send, xf_send, x_recv, q_send, q_recv,
-    ps_send, pr_recv, d_send, d_recv, r_send, r_recv, out_sem,
+    ps_send, pr_recv, d_send, d_recv, r_send, r_recv,
 ):
     n_seq, nz, nlq, plen, dlen, width, cols = cfg
     nx = n_seq // 2
@@ -307,16 +307,17 @@
     with scope("proj_own0"):
         project(x * 2, 2, 0, 1)
     with scope("q_fwd1"):
+        for ch in range(1, CHUNKS[0]):
+            forward(0, ch)
         if nz > 3:
             pass_q(2, 0)
     with scope("proj_own1"):
         project(x * 2, 2, 1, 2)
     with scope("fwd1"):
+        forward(1, 0)
         if nz > 3:
             for lq in range(1, nlq):
                 pass_q(2, lq)
-        for ch in range(1, CHUNKS[0]):
-            forward(0, ch)
         for ch in range(CHUNKS[0]):
             wait_other(0, ch)
     with scope("proj_a"):
@@ -350,13 +351,14 @@
             project_part(dx, ch)
 
     with scope("b01"):
-        forward(1, 0)
         forward(1, 1)
         take_part(0)
         take_part(1)
     with scope("b2"):
         forward(1, 2)
         take_part(2)
+    with scope("fwd3"):
+        forward(1, 3)
 
     low = lax.broadcasted_iota(jnp.int32, (dlen, 128), 1) < HD
 
@@ -394,8 +396,6 @@
             @pl.when(((b < z) & (z == nz - 1)) | ((b > z) & (z == 0)))
             def _():
                 q_copy(True, question).wait_recv()
-    with scope("fwd3"):
-        forward(1, 3)
     with scope("attend_own"):
         attend_all([x * 2, x * 2 + 1])
     with scope("attend_a"):
@@ -562,10 +562,11 @@
     with scope("chain"):
         for side in range(2):
             first_hop(side)
-        for k in range(nz - 1):
-            for side in range(2):
-                for lq in range(nlq):
-                    hop(side, k * nlq + lq)
+        for o in range(beyond + 1):
+            if o < beyond:
+                hop(0, o)
+            if o:
+                hop(1, o - 1)
 
     for half in range(2):
         to_partner(half).wait_send()
@@ -575,12 +576,12 @@
                 over_x(k, dx, ch).wait_send()
                 passed_on(k, dx, ch, c).wait_send()
 
-    order = list(range(1, nx)) + [0]
-
-    def product(lq, dest, h):
+
+    def product(lq, dest, first, count):
         src = pl.ds(pl.multiple_of(dest * piece, piece), piece)
-        heads = pl.ds(h * ppairs * 128, ppairs * 128)
-        return jnp.dot(att[lq, :, heads], ow_v[heads, src], preferred_element_type=F32)
+        heads = pl.ds(first * ppairs * 128, count * ppairs * 128)
+        rows_in = pl.ds(lq * dlen, dlen) if lq is not None else pl.ds(0, rows)
+        return jnp.dot(att[rows_in, heads], ow_v[heads, src], preferred_element_type=F32)
 
     def d_copy(lq, dx):
         return pltpu.make_async_remote_copy(
@@ -593,6 +594,21 @@
             src_ref=xsend.at[lq, dx], dst_ref=rx.at[lq, x], send_sem=r_send.at[lq, dx - 1],
             recv_sem=r_recv.at[lq, nx - 1 - dx], device_id={"seq": seq_of(dx, c)},
         )
+
+    def pair_sum(lq, dx):
+        d_copy(lq, dx).wait_recv()
+        both = rown[lq, dx] + dpart[lq, dx].astype(F32)
+        if dx:
+            xsend[lq, dx] = both.astype(BF16)
+            r_copy(lq, dx).start()
+        else:
+            mine = pl.ds(pl.multiple_of(me * piece, 128), piece)
+            rown[lq, 0] = both + dec_v[pl.ds(lq * dlen, dlen), mine].astype(F32)
+
+    def far_sums(lq):
+        with scope("pair_sum"):
+            for dx in range(1, nx):
+                pair_sum(lq, dx)
 
     for lq in range(nlq):
         def own_parts(h):
@@ -605,52 +621,50 @@
                 for i in range(h * ppairs // 2, (h + 1) * ppairs // 2):
                     t = jnp.transpose(jnp.concatenate([block(2 * i), block(2 * i + 1)], axis=0))
                     t = t.astype(BF16)
-                    att[lq, :, pl.ds(2 * i * 128, 128)] = t[:HD]
-                    att[lq, :, pl.ds((2 * i + 1) * 128, 128)] = t[HD:]
+                    att[pl.ds(lq * dlen, dlen), pl.ds(2 * i * 128, 128)] = t[:HD]
+                    att[pl.ds(lq * dlen, dlen), pl.ds((2 * i + 1) * 128, 128)] = t[HD:]
                 if lq == 0 and h == 0:
                     pltpu.make_async_copy(ow, ow_v, ow_sem.at[0]).wait()
 
         for h in range(parts - 1):
             own_parts(h)
             with scope("out_part"):
-                for n in range(n_seq):
-                    dest = seq_of(n // 2, (1 - c) if n % 2 == 0 else c)
-                    pacc[n] = product(lq, dest, h)
+                for dx in range(1, nx):
+                    for k in range(2):
+                        r = product(lq, seq_of(dx, (1 - c) if k == 0 else c), h, 1)
+                        pacc[2 * dx - 2 + k] = r + pacc[2 * dx - 2 + k] if h else r
         own_parts(parts - 1)
 
-        def pair_sum(dx):
-            d_copy(lq, dx).wait_recv()
-            both = rown[lq, dx] + dpart[lq, dx].astype(F32)
-            if dx:
-                xsend[lq, dx] = both.astype(BF16)
-                r_copy(lq, dx).start()
-            else:
-                mine = pl.ds(pl.multiple_of(me * piece, 128), piece)
-                rown[lq, 0] = both + dec_v[pl.ds(lq * dlen, dlen), mine].astype(F32)
-
         with scope("out"):
-            held = None
-            for n, dx in enumerate(order):
-                theirs = product(lq, seq_of(dx, 1 - c), parts - 1)
+            last = parts - 1
+            for dx in range(1, nx):
+                theirs = product(lq, seq_of(dx, 1 - c), last, 1)
+                held = product(lq, seq_of(dx, c), last, 1)
                 if parts > 1:
-                    theirs = theirs + pacc[2 * dx]
-                if held is not None:
-                    rown[lq, order[n - 1]] = held
-                held = product(lq, seq_of(dx, c), parts - 1)
-                if parts > 1:
-                    held = held + pacc[2 * dx + 1]
+                    theirs = theirs + pacc[2 * dx - 2]
+                    held = held + pacc[2 * dx - 1]
                 dsend[lq, dx] = theirs.astype(BF16)
                 d_copy(lq, dx).start()
-                if n > 1:
-                    pair_sum(order[n - 2])
-            rown[lq, order[-1]] = held
-        with scope("pair_sum"):
-            for dx in order[-2:]:
-                pair_sum(dx)
-    def out_copy(lq):
-        return pltpu.make_async_copy(
-            out_v.at[lq], out.at[pl.ds(lq * dlen, dlen)], out_sem.at[lq]
-        )
+                rown[lq, dx] = held
+        pl.when(c == 0)(functools.partial(far_sums, lq))
+
+    with scope("out_near"):
+        theirs = product(None, seq_of(0, 1 - c), 0, parts)
+        held = product(None, seq_of(0, c), 0, parts)
+        for lq in range(nlq):
+            dsend[lq, 0] = theirs[lq * dlen:(lq + 1) * dlen].astype(BF16)
+            d_copy(lq, 0).start()
+        for lq in range(nlq):
+            rown[lq, 0] = held[lq * dlen:(lq + 1) * dlen]
+
+    @pl.when(c == 1)
+    def _():
+        for lq in range(nlq):
+            far_sums(lq)
+
+    with scope("near_sum"):
+        for lq in range(nlq):
+            pair_sum(lq, 0)
 
     for d in range(2):
         for o in range(beyond):
@@ -673,12 +687,10 @@
                     recv_sem=r_recv.at[lq, dx - 1], device_id={"seq": xs * 2 + c},
                 ).wait_recv()
                 total = total + rx[lq, xs].astype(F32)
-            out_v[lq] = total.astype(BF16)
-            out_copy(lq).start()
+            out[pl.ds(lq * dlen, dlen), :] = total.astype(BF16)
     for lq in range(nlq):
         for dx in range(1, nx):
             r_copy(lq, dx).wait_send()
-        out_copy(lq).wait()
 
 
 def body(
@@ -703,10 +715,10 @@
     dma = pltpu.SemaphoreType.DMA
     result = pl.pallas_call(
         functools.partial(kernel, cfg),
-        out_shape=jax.ShapeDtypeStruct((rows, piece), BF16),
+        out_shape=pltpu.VMEM((rows, piece), BF16),
         in_specs=[pl.BlockSpec(memory_space=pltpu.SMEM), any_spec, any_spec, any_spec, any_spec,
                   any_spec, any_spec, any_spec],
-        out_specs=any_spec,
+        out_specs=pl.BlockSpec(memory_space=pltpu.VMEM),
         scratch_shapes=[
             pltpu.VMEM((width,), BF16),
             pltpu.VMEM((width,), BF16),
@@ -726,7 +738,7 @@
             pltpu.VMEM((2, beyond, half + 32, 128), BF16),
             pltpu.VMEM((2, beyond, half + 32, 128), BF16),
             pltpu.VMEM((2, half + 32, 128), BF16),
-            pltpu.VMEM((nlq, dlen, cols), BF16),
+            pltpu.VMEM((rows, cols), BF16),
             pltpu.VMEM((nlq, nx, dlen, piece), BF16),
             pltpu.VMEM((nlq, nx, dlen, piece), BF16),
             pltpu.VMEM((nlq, nx, dlen, piece), BF16),
@@ -735,13 +747,12 @@
             pltpu.VMEM((2 * cols // 128, plen, 128), F32),
             pltpu.VMEM((2 * cols // 128, plen, 128), BF16),
             pltpu.VMEM((max(8, 2 * cols // 128), 128), F32),
-            pltpu.VMEM((nlq, dlen, piece), BF16),
             pltpu.VMEM((nx - 1, plen, 2 * cols), F32),
-            pltpu.VMEM((n_seq, dlen, piece) if cols % 512 == 0 else (1, 8, 128), F32),
+            pltpu.VMEM((n_seq - 2, dlen, piece) if cols % 512 == 0 else (1, 8, 128), F32),
             dma((6,)), dma((slots,)), dma((1,)),
             dma((2,)), dma((2,)), dma((nx - 1, nch)), dma((nx - 1, nch)), dma((nx - 1, 2, nch)),
             dma((2, nq)), dma((nq,)), dma((2, beyond, parts)), dma((2, beyond, parts)),
-            dma((nlq, nx)), dma((nlq, nx)), dma((nlq, nx - 1)), dma((nlq, nx - 1)), dma((nlq,)),
+            dma((nlq, nx)), dma((nlq, nx)), dma((nlq, nx - 1)), dma((nlq, nx - 1)),
         ],
         compiler_params=pltpu.CompilerParams(
             collective_id=0, has_side_effects=True, vmem_limit_bytes=63 * 1024 * 1024

time: 60.5 us -> 57.2 us (0.945)
  the two profiles are of different devices: /device:TPU:20 before, /device:TPU:0 now
where the time goes in v3:
time: 57.2 us; the launch traced here: 56.4 us
  Pallas kernels  55.7 us (97%)
  local copies, waits for them, and re-layouts  0.71 us (1%)
    pallas_call x1, Pallas kernels, body(): pl.pallas_call(functools.partial(kernel, cfg), out_shape=pltpu.VMEM((rows...  55.7 us

profile of v3, /device:TPU:0, one launch (start us, length us, event | category | flops | bytes accessed | tf_op | source)
XLA Modules:
  0.0 56.4 jit_solution(12912244126683292667)
XLA Ops:
  0.0 55.7 %reader.1 = bf16[128,1024]{1,0:T(8,128)(2,1)S(1)} custom-call(s32[4,4]{1,0:T(4,128)} %bitcast.7, bf16[128,4096]{1,0:T(8,128)(2,1)} %bitcast.5, bf16[4096]{0:T(1024)(128)(2,1)} %enc_gain.1, bf16[128,4096]{1,0:T(8,128)(2,1)} %bitcast.6, bf16[4096]{0:T(1024)(128)(2,1)} %dec_gain.1, bf16[4096,1024]{1,0:T(8,128)(2,1)} %qw.1, bf16[4096,2,1024]{2,1,0:T(2,128)(2,1)} %kvw.1, ...), custom_call_target="tpu_custom_call" | custom-call | tf_op jit(solution)/shard_map/reader/pallas_call | solution.py:716
  55.7 0.7 %copy.10 = bf16[2,64,1024]{2,1,0:T(8,128)(2,1)} copy(bf16[2,64,1024]{2,1,0:T(8,128)(2,1)S(1)} %bitcast.4) | data formatting | bytes 524288

commit v4 on v3

--- a/solution.py
+++ b/solution.py
@@ -9,7 +9,8 @@
 HD = 64
 EPSILON = 1e-06
 DEAD = -1e30
-CHUNKS = (2, 4)
+EIGHTHS = ((4, 4), (2, 2, 2, 1, 1))
+CHUNKS = tuple(len(t) for t in EIGHTHS)
 KT = 1024
 F32 = jnp.float32
 BF16 = jnp.bfloat16
@@ -30,11 +31,11 @@
 
 
 def kernel(
-    cfg, qo, states, enc_gain, dec_states, dec_gain, qw, kvw, ow, out,
-    eg_v, dg_v, xin, dec_v, gat, qw_v, raw, pulled, kv_v, ow_v, xn, kvs, qall, a_s, e_s,
+    cfg, qo_in, states, enc_gain, dec_states, dec_gain, qw, kvw, ow, out,
+    qo, eg_v, dg_v, xin, dec_v, gat, qw_v, raw, pulled, kv_v, ow_v, xn, kvs, qall, a_s, e_s,
     ps, pr, pick, att, dsend, dpart, xsend, rx, rown, s_buf, w_buf, i_buf, acc, pacc,
     local_sem, raw_sem, ow_sem, xp_send, xp_recv, xs_send, xf_send, x_recv, q_send, q_recv,
-    ps_send, pr_recv, d_send, d_recv, r_send, r_recv,
+    pr_recv, d_send, d_recv, r_send, r_recv,
 ):
     n_seq, nz, nlq, plen, dlen, width, cols = cfg
     nx = n_seq // 2
@@ -85,6 +86,8 @@
     dg_copy.start()
     dec_copy = pltpu.make_async_copy(dec_states, dec_v, local_sem.at[4])
     dec_copy.start()
+    qo_copy = pltpu.make_async_copy(qo_in, qo, local_sem.at[6])
+    qo_copy.start()
     qw_copy = pltpu.make_async_copy(qw, qw_v, local_sem.at[5])
     qw_copy.start()
     nblocks = cols // 128
@@ -140,11 +143,12 @@
             device_id={"seq": partner},
         )
 
+    def columns(k, ch):
+        eighth = width // 8
+        return pl.ds(sum(EIGHTHS[k][:ch]) * eighth, EIGHTHS[k][ch] * eighth)
+
     def x_copy(slot, half, k, ch, to, send_sem, source):
-        wide = width // CHUNKS[k]
-        part = gat.at[
-            slot, pl.ds(pl.multiple_of(half * hr, hr), hr), pl.ds(ch * wide, wide)
-        ]
+        part = gat.at[slot, pl.ds(pl.multiple_of(half * hr, hr), hr), columns(k, ch)]
         return pltpu.make_async_remote_copy(
             src_ref=part, dst_ref=part, send_sem=send_sem,
             recv_sem=x_recv.at[source, half, k * CHUNKS[0] + ch], device_id={"seq": to},
@@ -327,15 +331,12 @@
         for j in range(3, nz - 1):
             for lq in range(nlq):
                 pass_q(j, lq)
-    wide = width // CHUNKS[1]
-
-    def project_part(dx, ch):
+    def project_part(dx, ch, starts, tile):
         p = seq_of(dx, 1)
-        tile = min(KT, cols)
-        for i in range(2 * cols // tile):
-            at = pl.ds(i * tile, tile)
+        for start in starts:
+            at = pl.ds(start, tile)
             r = jnp.dot(
-                gat[p, :, pl.ds(ch * wide, wide)], kv_v[pl.ds(ch * wide, wide), at],
+                gat[p, :, columns(1, ch)], kv_v[columns(1, ch), at],
                 preferred_element_type=F32,
             )
             if ch:
@@ -348,7 +349,7 @@
     def take_part(ch):
         wait_other(1, ch)
         for dx in range(1, nx):
-            project_part(dx, ch)
+            project_part(dx, ch, (0, cols), cols)
 
     with scope("b01"):
         forward(1, 1)
@@ -356,14 +357,13 @@
         take_part(1)
     with scope("b2"):
         forward(1, 2)
+        forward(1, 3)
         take_part(2)
-    with scope("fwd3"):
-        forward(1, 3)
 
     low = lax.broadcasted_iota(jnp.int32, (dlen, 128), 1) < HD
 
-    def attend_all(ps_list):
-        units = [(u * npairs + j, p, j) for u, p in enumerate(ps_list) for j in range(npairs)]
+    def attend_all(ps_list, pairs=range(npairs)):
+        units = [(u * len(pairs) + i, p, j) for u, p in enumerate(ps_list) for i, j in enumerate(pairs)]
         for n, p, j in units:
             q = qall[qo[z, p], :, pl.ds(j * 128, 128)]
             zero = jnp.zeros_like(q)
@@ -379,7 +379,7 @@
             l = jnp.sum(w, axis=0, keepdims=True)
             w_buf[n] = w.astype(BF16)
             i_buf[pl.ds(n, 1), :] = 1.0 / l
-            e_s[p, pl.ds(j, 1), :] = m + jnp.log(l)
+            e_s[p, j // ppairs, pl.ds(j % ppairs, 1), :] = m + jnp.log(l)
         for n, p, j in units:
             o = lax.dot_general(
                 kvs[p, :, pl.ds(cols + j * 128, 128)], w_buf[n], (((0,), (0,)), ((), ())),
@@ -387,9 +387,11 @@
             )
             a_s[p, pl.ds(j * HD, HD), :] = jnp.where(low, o[:HD], o[HD:]) * i_buf[n:n + 1, :]
 
-    if npairs < 8:
-        e_s[...] = jnp.zeros(e_s.shape, F32)
+    e_s[...] = jnp.zeros(e_s.shape, F32)
+    with scope("fwd4"):
+        forward(1, 4)
     with scope("wait_q"):
+        qo_copy.wait()
         for question in range(nlq * nz):
             b = question // nlq
 
@@ -398,27 +400,27 @@
                 q_copy(True, question).wait_recv()
     with scope("attend_own"):
         attend_all([x * 2, x * 2 + 1])
+    with scope("b_3"):
+        take_part(3)
     with scope("attend_a"):
         for dx in range(1, nx):
             attend_all([seq_of(dx, 0)])
 
-    def put_logs(ref, e):
-        hi = e.astype(BF16)
-        rest = e - hi.astype(F32)
-        mid = rest.astype(BF16)
-        lo = (rest - mid.astype(F32)).astype(BF16)
-        ref[pl.ds(prows, 16), :] = jnp.concatenate([hi, mid], axis=0)
-        ref[pl.ds(prows + 16, 16), :] = jnp.concatenate([lo, jnp.zeros_like(lo)], axis=0)
-
-    def get_logs(ref):
-        two = ref[pl.ds(prows, 16), :].astype(F32)
-        return two[:8] + two[8:] + ref[pl.ds(prows + 16, 16), :].astype(F32)[:8]
-
-    with scope("b3"):
-        take_part(3)
-    with scope("attend_b"):
-        for dx in range(1, nx):
-            attend_all([seq_of(dx, 1)])
+    erows = 16
+
+    def put_logs(ref, e, h):
+        hi = e.astype(BF16).astype(F32)
+        rest = e - hi
+        mid = rest.astype(BF16).astype(F32)
+        pieces = [t[:ppairs] for t in (hi, mid, rest - mid)]
+        pieces.append(jnp.zeros((erows - 3 * ppairs, 128), F32))
+        at = pl.ds(h * (prows + erows) + prows, erows)
+        ref[at, :] = jnp.concatenate(pieces, axis=0).astype(BF16)
+
+    def get_logs(ref, h):
+        t = ref[pl.ds(h * (prows + erows) + prows, erows), :].astype(F32)
+        e = t[:ppairs] + t[ppairs:2 * ppairs] + t[2 * ppairs:3 * ppairs]
+        return jnp.concatenate([e, jnp.zeros((8 - ppairs, 128), F32)], axis=0)
 
     near = (2 * z >= nz).astype(jnp.int32)
     sides = (near, 1 - near)
@@ -440,7 +442,7 @@
 
     plans = [packing(d) for d in sides]
 
-    def terms(question, sources):
+    def terms(question, sources, h):
         first = jnp.int32(0)
         second = jnp.int32(0)
         count = jnp.int32(0)
@@ -449,8 +451,8 @@
             first = jnp.where(hit & (count == 0), p, first)
             second = jnp.where(hit & (count == 1), p, second)
             count = count + hit.astype(jnp.int32)
-        e = [jnp.where(count >= 1, e_s[first], DEAD), jnp.where(count >= 2, e_s[second], DEAD)]
-        e += [jnp.where(ok, get_logs(pick.at[side]), DEAD) for side, ok in sources]
+        e = [jnp.where(count >= 1, e_s[first, h], DEAD), jnp.where(count >= 2, e_s[second, h], DEAD)]
+        e += [jnp.where(ok, get_logs(pick.at[side], h), DEAD) for side, ok in sources]
         top = functools.reduce(jnp.maximum, e)
         w = [jnp.exp(t - top) for t in e]
         tot = functools.reduce(jnp.add, w)
@@ -459,22 +461,22 @@
 
         def block(j):
             at = pl.ds(j * HD, HD)
-            there = pl.ds(j * HD + (32 if j >= ppairs else 0), HD)
+            there = pl.ds(j * HD + erows * h, HD)
             values = [a_s[first, at, :], a_s[second, at, :]]
             values += [pick[side, there, :].astype(F32) for side, ok in sources]
             return functools.reduce(
-                jnp.add, [t * u[j:j + 1, :] for t, u in zip(values, w, strict=True)]
+                jnp.add, [t * u[j - h * ppairs:j - h * ppairs + 1, :] for t, u in zip(values, w, strict=True)]
             )
 
         return block, top + jnp.log(tot)
 
     def part_rows(h):
-        return pl.ds(0, prows + 32) if h == 0 else pl.ds(prows + 32, prows)
+        return pl.ds(h * (prows + erows), prows + erows)
 
     def result_copy(d, n, h):
         at = part_rows(h)
         return pltpu.make_async_remote_copy(
-            src_ref=ps.at[d, n, at], dst_ref=pr.at[d, n, at], send_sem=ps_send.at[d, n, h],
+            src_ref=ps.at[d, n, at], dst_ref=pr.at[d, n, at], send_sem=q_send.at[d, n * parts + h],
             recv_sem=pr_recv.at[d, n, h], device_id={"qset": z + 1 - 2 * d},
         )
 
@@ -515,40 +517,40 @@
         _, found = plans[side]
         return ~at_edge(d) & (~after_edge(d) | (found[packed_o] > 0))
 
-    def put_slot(d, n, block, e, h):
+    def put_slot(d, n, question, sources, h):
+        block, e = terms(question, sources, h)
         for j in range(h * ppairs, (h + 1) * ppairs):
-            ps[d, n, pl.ds(j * HD + (32 if h else 0), HD), :] = block(j).astype(BF16)
-        if h == 0:
-            put_logs(ps.at[d, n], e)
+            ps[d, n, pl.ds(j * HD + erows * h, HD), :] = block(j).astype(BF16)
+        put_logs(ps.at[d, n], e, h)
         result_copy(d, n, h).start()
 
-    def first_hop(side):
+    def nth_found(side, n):
+        ranks, found = plans[side]
+        question = jnp.int32(-1)
+        rank = jnp.int32(0)
+        for o in range(beyond):
+            question = jnp.where(
+                (found[o] > 0) & (rank == n), question_at(sides[side], o), question
+            )
+            rank = rank + found[o]
+        return question
+
+    def first_hop(side, todo):
         d = sides[side]
-        ranks, found = plans[side]
 
         @pl.when(at_edge(d))
         def _():
-            for n in range(packed):
-                question = jnp.int32(-1)
-                rank = jnp.int32(0)
-                for o in range(beyond):
-                    question = jnp.where((found[o] > 0) & (rank == n), question_at(d, o), question)
-                    rank = rank + found[o]
-                block, e = terms(question, [])
-                for h in range(parts):
-                    put_slot(d, n, block, e, h)
+            for n, h in todo:
+                put_slot(d, n, nth_found(side, n), [], h)
 
     def hop(side, o):
         d = sides[side]
 
         @pl.when((o < places(d)) & ~at_edge(d))
         def _():
-            take(side, o, o, 0)
-            block, e = terms(question_at(d, o), [(side, have(side, o))])
-            put_slot(d, o, block, e, 0)
-            for h in range(1, parts):
+            for h in range(parts):
                 take(side, o, o, h)
-                put_slot(d, o, block, e, h)
+                put_slot(d, o, question_at(d, o), [(side, have(side, o))], h)
 
     for question in range(nlq * nz):
         @pl.when(up_ok & (question // nlq <= z))
@@ -559,9 +561,21 @@
         def _():
             q_copy(False, question).wait_send()
 
+    todo = [(n, h) for n in range(packed) for h in range(parts)]
+    with scope("b3"):
+        wait_other(1, CHUNKS[1] - 1)
+    span = cols // parts
+    for h in range(parts):
+        with scope("b3"):
+            for dx in range(1, nx):
+                project_part(dx, CHUNKS[1] - 1, (h * span, cols + h * span), span)
+        with scope("attend_b"):
+            for dx in range(1, nx):
+                attend_all([seq_of(dx, 1)], range(h * ppairs, (h + 1) * ppairs))
+            for side in range(2):
+                first_hop(side, todo[:1] if h < parts - 1 else todo[min(parts - 1, 1):])
+
     with scope("chain"):
-        for side in range(2):
-            first_hop(side)
         for o in range(beyond + 1):
             if o < beyond:
                 hop(0, o)
@@ -617,7 +631,7 @@
                 for side in range(2):
                     take(side, places(sides[side]) + lq, last, h)
             with scope("finish"):
-                block, _ = terms(z * nlq + lq, [(side, have(side, last)) for side in range(2)])
+                block, _ = terms(z * nlq + lq, [(side, have(side, last)) for side in range(2)], h)
                 for i in range(h * ppairs // 2, (h + 1) * ppairs // 2):
                     t = jnp.transpose(jnp.concatenate([block(2 * i), block(2 * i + 1)], axis=0))
                     t = t.astype(BF16)
@@ -646,7 +660,7 @@
                 dsend[lq, dx] = theirs.astype(BF16)
                 d_copy(lq, dx).start()
                 rown[lq, dx] = held
-        pl.when(c == 0)(functools.partial(far_sums, lq))
+        far_sums(lq)
 
     with scope("out_near"):
         theirs = product(None, seq_of(0, 1 - c), 0, parts)
@@ -656,11 +670,6 @@
             d_copy(lq, 0).start()
         for lq in range(nlq):
             rown[lq, 0] = held[lq * dlen:(lq + 1) * dlen]
-
-    @pl.when(c == 1)
-    def _():
-        for lq in range(nlq):
-            far_sums(lq)
 
     with scope("near_sum"):
         for lq in range(nlq):
@@ -716,10 +725,11 @@
     result = pl.pallas_call(
         functools.partial(kernel, cfg),
         out_shape=pltpu.VMEM((rows, piece), BF16),
-        in_specs=[pl.BlockSpec(memory_space=pltpu.SMEM), any_spec, any_spec, any_spec, any_spec,
+        in_specs=[any_spec, any_spec, any_spec, any_spec, any_spec,
                   any_spec, any_spec, any_spec],
         out_specs=pl.BlockSpec(memory_space=pltpu.VMEM),
         scratch_shapes=[
+            pltpu.SMEM((nz, n_seq), jnp.int32),
             pltpu.VMEM((width,), BF16),
             pltpu.VMEM((width,), BF16),
             pltpu.VMEM((plen, width), BF16),
@@ -734,10 +744,10 @@
             pltpu.VMEM((n_seq, plen, 2 * cols), BF16),
             pltpu.VMEM((nq, dlen, cols), BF16),
             pltpu.VMEM((n_seq, half, 128), F32),
-            pltpu.VMEM((n_seq, 8, 128), F32),
-            pltpu.VMEM((2, beyond, half + 32, 128), BF16),
-            pltpu.VMEM((2, beyond, half + 32, 128), BF16),
-            pltpu.VMEM((2, half + 32, 128), BF16),
+            pltpu.VMEM((n_seq, parts, 8, 128), F32),
+            pltpu.VMEM((2, beyond, half + 16 * parts, 128), BF16),
+            pltpu.VMEM((2, beyond, half + 16 * parts, 128), BF16),
+            pltpu.VMEM((2, half + 16 * parts, 128), BF16),
             pltpu.VMEM((rows, cols), BF16),
             pltpu.VMEM((nlq, nx, dlen, piece), BF16),
             pltpu.VMEM((nlq, nx, dlen, piece), BF16),
@@ -749,9 +759,9 @@
             pltpu.VMEM((max(8, 2 * cols // 128), 128), F32),
             pltpu.VMEM((nx - 1, plen, 2 * cols), F32),
             pltpu.VMEM((n_seq - 2, dlen, piece) if cols % 512 == 0 else (1, 8, 128), F32),
-            dma((6,)), dma((slots,)), dma((1,)),
+            dma((7,)), dma((slots,)), dma((1,)),
             dma((2,)), dma((2,)), dma((nx - 1, nch)), dma((nx - 1, nch)), dma((nx - 1, 2, nch)),
-            dma((2, nq)), dma((nq,)), dma((2, beyond, parts)), dma((2, beyond, parts)),
+            dma((2, max(nq, beyond * parts))), dma((nq,)), dma((2, beyond, parts)),
             dma((nlq, nx)), dma((nlq, nx)), dma((nlq, nx - 1)), dma((nlq, nx - 1)),
         ],
         compiler_params=pltpu.CompilerParams(

time: 57.2 us -> 55.7 us (0.974); the launches traced: 56.4 us -> 55.5 us
  Pallas kernels: 55.7 us -> 54.8 us
    pallas_call x1, Pallas kernels: 55.7 us -> 54.8 us  [body(): pl.pallas_call(functools.partial(kernel, cfg), out_shape=pltpu.VMEM((rows...]
where the time goes in v4:
time: 55.7 us; the launch traced here: 55.5 us
  Pallas kernels  54.8 us (98%)
  local copies, waits for them, and re-layouts  0.71 us (1%)
    pallas_call x1, Pallas kernels, body(): pl.pallas_call(functools.partial(kernel, cfg), out_shape=pltpu.VMEM((rows...  54.8 us

profile of v4, /device:TPU:0, one launch (start us, length us, event | category | flops | bytes accessed | tf_op | source)
XLA Modules:
  0.0 55.5 jit_solution(16244493148266427090)
XLA Ops:
  0.0 54.8 %reader.1 = bf16[128,1024]{1,0:T(8,128)(2,1)S(1)} custom-call(s32[4,4]{1,0:T(4,128)} %bitcast.7, bf16[128,4096]{1,0:T(8,128)(2,1)} %bitcast.5, bf16[4096]{0:T(1024)(128)(2,1)} %enc_gain.1, bf16[128,4096]{1,0:T(8,128)(2,1)} %bitcast.6, bf16[4096]{0:T(1024)(128)(2,1)} %dec_gain.1, bf16[4096,1024]{1,0:T(8,128)(2,1)} %qw.1, bf16[4096,2,1024]{2,1,0:T(2,128)(2,1)} %kvw.1, ...), custom_call_target="tpu_custom_call" | custom-call | tf_op jit(solution)/shard_map/reader/pallas_call | solution.py:725
  54.8 0.7 %copy.10 = bf16[2,64,1024]{2,1,0:T(8,128)(2,1)} copy(bf16[2,64,1024]{2,1,0:T(8,128)(2,1)S(1)} %bitcast.4) | data formatting | bytes 524288

commit v5 on v4

--- a/solution.py
+++ b/solution.py
@@ -355,11 +355,6 @@
         forward(1, 1)
         take_part(0)
         take_part(1)
-    with scope("b2"):
-        forward(1, 2)
-        forward(1, 3)
-        take_part(2)
-
     low = lax.broadcasted_iota(jnp.int32, (dlen, 128), 1) < HD
 
     def attend_all(ps_list, pairs=range(npairs)):
@@ -388,8 +383,8 @@
             a_s[p, pl.ds(j * HD, HD), :] = jnp.where(low, o[:HD], o[HD:]) * i_buf[n:n + 1, :]
 
     e_s[...] = jnp.zeros(e_s.shape, F32)
-    with scope("fwd4"):
-        forward(1, 4)
+    with scope("fwd2"):
+        forward(1, 2)
     with scope("wait_q"):
         qo_copy.wait()
         for question in range(nlq * nz):
@@ -398,13 +393,18 @@
             @pl.when(((b < z) & (z == nz - 1)) | ((b > z) & (z == 0)))
             def _():
                 q_copy(True, question).wait_recv()
+    with scope("attend_a"):
+        for dx in range(1, nx):
+            attend_all([seq_of(dx, 0)])
+    with scope("b2"):
+        forward(1, 3)
+        take_part(2)
+    with scope("fwd4"):
+        forward(1, 4)
     with scope("attend_own"):
         attend_all([x * 2, x * 2 + 1])
     with scope("b_3"):
         take_part(3)
-    with scope("attend_a"):
-        for dx in range(1, nx):
-            attend_all([seq_of(dx, 0)])
 
     erows = 16
 
@@ -647,6 +647,8 @@
                     for k in range(2):
                         r = product(lq, seq_of(dx, (1 - c) if k == 0 else c), h, 1)
                         pacc[2 * dx - 2 + k] = r + pacc[2 * dx - 2 + k] if h else r
+        if lq:
+            pl.when(c == 1)(functools.partial(far_sums, lq - 1))
         own_parts(parts - 1)
 
         with scope("out"):
@@ -660,7 +662,10 @@
                 dsend[lq, dx] = theirs.astype(BF16)
                 d_copy(lq, dx).start()
                 rown[lq, dx] = held
-        far_sums(lq)
+        if lq < nlq - 1:
+            pl.when(c == 0)(functools.partial(far_sums, lq))
+        else:
+            far_sums(lq)
 
     with scope("out_near"):
         theirs = product(None, seq_of(0, 1 - c), 0, parts)

time: 55.7 us -> 55.7 us (level)
  the two profiles are of different devices: /device:TPU:0 before, /device:TPU:9 now
where the time goes in v5:
time: 55.7 us; the launch traced here: 55.5 us
  Pallas kernels  54.8 us (98%)
  local copies, waits for them, and re-layouts  0.71 us (1%)
    pallas_call x1, Pallas kernels, body(): pl.pallas_call(functools.partial(kernel, cfg), out_shape=pltpu.VMEM((rows...  54.8 us

profile of v5, /device:TPU:9, one launch (start us, length us, event | category | flops | bytes accessed | tf_op | source)
XLA Modules:
  0.0 55.5 jit_solution(10266633492815442670)
XLA Ops:
  0.0 54.8 %reader.1 = bf16[128,1024]{1,0:T(8,128)(2,1)S(1)} custom-call(s32[4,4]{1,0:T(4,128)} %bitcast.7, bf16[128,4096]{1,0:T(8,128)(2,1)} %bitcast.5, bf16[4096]{0:T(1024)(128)(2,1)} %enc_gain.1, bf16[128,4096]{1,0:T(8,128)(2,1)} %bitcast.6, bf16[4096]{0:T(1024)(128)(2,1)} %dec_gain.1, bf16[4096,1024]{1,0:T(8,128)(2,1)} %qw.1, bf16[4096,2,1024]{2,1,0:T(2,128)(2,1)} %kvw.1, ...), custom_call_target="tpu_custom_call" | custom-call | tf_op jit(solution)/shard_map/reader/pallas_call | solution.py:730
  54.8 0.7 %copy.10 = bf16[2,64,1024]{2,1,0:T(8,128)(2,1)} copy(bf16[2,64,1024]{2,1,0:T(8,128)(2,1)S(1)} %bitcast.4) | data formatting | bytes 524288
